TPU v7x, 128 devices: a whole 4x4x4 slice. The times are simulated.
128 devices in a mesh: gx: 2 (over core), gy: 64 (over z, y, x).
Axes of the slice: x: 4, y: 4, z: 4, core: 2. Of those that a mesh axis runs over, the one named last changes fastest.
Arguments:
- right_side: float32 [128, 16384], P('gx', 'gy'), may hold values from -34 to 34, as said below
- initial: float32 [128, 16384], P('gx', 'gy'), may hold values from -0.6 to 0.6
- reaction: float32 [128, 16384], P('gx', 'gy'), may hold values from 0.05 to 0.5
- velocity_x: float32 [128, 16384], P('gx', 'gy'), may hold values from -1 to 1
- velocity_y: float32 [128, 16384], P('gx', 'gy'), may hold values from -1 to 1
Outputs:
- solution: float32 [128, 16384], P('gx', 'gy')
- residual: float32 [128, 16384], P('gx', 'gy')
Inputs may be any that keep to these rules, and one draw needn't show every extreme that they name: right_side is noise bounded by 4 in size times an envelope 0.5 + 8 g, where g is a periodic Gaussian bump of one device block's width along each dimension centred at a drawn position, so its entries lie within -34 and 34.
All inputs are finite; a program needn't handle non-finite values.
Results may differ from a plain program's by a relative error of at most 0.0075.
Values sent between devices are 32-bit elements.
No kernel may reach another device: no remote copies, remote signals or barrier semaphores. Data moves between devices by JAX's collectives and lax.ppermute only.
A program may use at most 64 MiB of HBM per device.

v0:
```python
import jax
import jax.numpy as jnp
from jax import lax
from jax.sharding import Mesh
from jax.sharding import PartitionSpec as P

RESTART = 15
GX_GY = ("gx", "gy_0", "gy_1", "gy_2")
GY = ("gy_0", "gy_1", "gy_2")


def padded_2(cells, sides, width, closed):
    for axis, dim in sides:
        count = lax.axis_size(axis)
        ends = count if closed else count - 1
        head = lax.slice_in_dim(cells, 0, width, axis=dim)
        tail = lax.slice_in_dim(cells, cells.shape[dim] - width, cells.shape[dim], axis=dim)
        cells = jnp.concatenate(
            [
                lax.ppermute(tail, axis, [(i, (i + 1) % count) for i in range(ends)]),
                cells,
                lax.ppermute(head, axis, [((i + 1) % count, i) for i in range(ends)]),
            ],
            axis=dim,
        )
    return cells


def one_axis_at_a_time(x, axes):
    for axis in axes:
        x = lax.psum(x, axis)
    return x


def shifted(padded, offset, dimension, extent):
    row_start = 2 + offset if dimension == 0 else 2
    column_start = 2 + offset if dimension == 1 else 2
    return lax.slice(
        padded, (row_start, column_start), (row_start + extent[0], column_start + extent[1])
    )


def first_diff(padded, dimension, extent):
    outer = shifted(padded, -2, dimension, extent) - shifted(padded, 2, dimension, extent)
    inner = shifted(padded, 1, dimension, extent) - shifted(padded, -1, dimension, extent)
    return (outer + 8.0 * inner) / 12.0


def second_diff(padded, dimension, extent):
    inner = shifted(padded, 1, dimension, extent) + shifted(padded, -1, dimension, extent)
    outer = shifted(padded, 2, dimension, extent) + shifted(padded, -2, dimension, extent)
    return (16.0 * inner - outer - 30.0 * shifted(padded, 0, dimension, extent)) / 12.0


def apply_operator(field, padded_field, padded_speeds, reaction, velocity_x, velocity_y):
    extent = field.shape
    diffusion = second_diff(padded_field, 0, extent) + second_diff(padded_field, 1, extent)
    advect_x = 0.5 * (
        velocity_x * first_diff(padded_field, 0, extent)
        + first_diff(padded_speeds[0] * padded_field, 0, extent)
    )
    advect_y = 0.5 * (
        velocity_y * first_diff(padded_field, 1, extent)
        + first_diff(padded_speeds[1] * padded_field, 1, extent)
    )
    return reaction * field - diffusion + advect_x + advect_y


def least_squares(hessenberg, beta):
    columns_total = hessenberg.shape[1]
    target = jnp.where(jnp.arange(columns_total + 1) == 0, beta, 0.0)

    def rotate(column, carried):
        upper, target = carried
        top_row = upper[column]
        next_row = upper[column + 1]
        diagonal_entry = top_row[column]
        below_entry = next_row[column]
        radius = jnp.sqrt(diagonal_entry * diagonal_entry + below_entry * below_entry)
        cosine = diagonal_entry / radius
        sine_value = below_entry / radius
        upper = upper.at[column].set(cosine * top_row + sine_value * next_row)
        upper = upper.at[column + 1].set(cosine * next_row - sine_value * top_row)
        upper_value = target[column]
        lower_value = target[column + 1]
        target = target.at[column].set(cosine * upper_value + sine_value * lower_value)
        target = target.at[column + 1].set(cosine * lower_value - sine_value * upper_value)
        return (upper, target)

    upper, target = lax.fori_loop(0, columns_total, rotate, (hessenberg, target))

    def substitute(count, weights):
        row_index = columns_total - 1 - count
        known = jnp.sum(upper[row_index] * weights)
        return weights.at[row_index].set((target[row_index] - known) / upper[row_index, row_index])

    return lax.fori_loop(0, columns_total, substitute, jnp.zeros((columns_total,), jnp.float32))


def per_device(right_side, initial, reaction, velocity_x, velocity_y):
    row_count, column_count = right_side.shape
    speeds = jnp.stack([velocity_x, velocity_y])
    padded_speeds = padded_2(speeds, (("gx", 1), (GY, 2)), 2, True)

    def operator_on(field):
        padded_field = padded_2(field, (("gx", 0), (GY, 1)), 2, True)
        return apply_operator(field, padded_field, padded_speeds, reaction, velocity_x, velocity_y)

    start_residual = right_side - operator_on(initial)
    start_square = one_axis_at_a_time(jnp.sum(start_residual * start_residual), GX_GY)
    beta = jnp.sqrt(start_square)
    basis = jnp.zeros((RESTART + 1, row_count, column_count), jnp.float32)
    basis = basis.at[0].set(start_residual / beta)
    hessenberg = jnp.zeros((RESTART + 1, RESTART), jnp.float32)
    positions = jnp.arange(RESTART + 1)

    def arnoldi(column, carried):
        basis, hessenberg = carried
        current = lax.dynamic_index_in_dim(basis, column, 0, keepdims=False)
        applied = operator_on(current)
        local_projection = jnp.einsum("kxy,xy->k", basis, applied, precision=lax.Precision.HIGHEST)
        projection, applied_square = (
            one_axis_at_a_time(local_projection, GX_GY),
            one_axis_at_a_time(jnp.sum(applied * applied), GX_GY),
        )
        applied = applied - jnp.einsum(
            "k,kxy->xy", projection, basis, precision=lax.Precision.HIGHEST
        )
        length = jnp.sqrt(applied_square - jnp.sum(projection * projection))
        entries = jnp.where(positions == column + 1, length, projection)
        hessenberg = lax.dynamic_update_slice(hessenberg, entries[:, None], (0, column))
        basis = lax.dynamic_update_index_in_dim(basis, applied / length, column + 1, 0)
        return (basis, hessenberg)

    basis, hessenberg = lax.fori_loop(0, RESTART, arnoldi, (basis, hessenberg))
    weights = least_squares(hessenberg, beta)
    padded_weights = jnp.concatenate([weights, jnp.zeros((1,), jnp.float32)])
    solution = initial + jnp.einsum(
        "k,kxy->xy", padded_weights, basis, precision=lax.Precision.HIGHEST
    )
    leftover = jnp.where(positions == 0, beta, 0.0) - jnp.dot(
        hessenberg, weights, precision=lax.Precision.HIGHEST
    )
    residual = jnp.einsum("k,kxy->xy", leftover, basis, precision=lax.Precision.HIGHEST)
    return (solution, residual)


def solution(mesh):
    torus = Mesh(mesh.devices.reshape(mesh.shape["gx"], 4, 4, 4), ("gx", "gy_0", "gy_1", "gy_2"))
    placed = (P("gx", GY), P("gx", GY), P("gx", GY), P("gx", GY), P("gx", GY))
    return jax.shard_map(
        per_device,
        mesh=torus,
        in_specs=placed,
        out_specs=(P("gx", GY), P("gx", GY)),
        check_vma=False,
    )
```

profile of v0, /device:TPU:1, one launch (start us, length us, event | category | flops | bytes accessed | tf_op | source)
XLA Modules:
  0.0 1030.0 jit_solution(6680681950074222786)
XLA Ops:
  4.6 8.6 collective-permute-start.6
  13.4 7.0 collective-permute-start.11
  42.7 13.4 %psum.143 = f32[]{:T(128)} all-reduce(f32[]{:T(128)} %psum.142), channel_id=1, replica_groups=mesh['gx'=2,'gy_0'=4,'gy_1'=4,'gy_2'=4] {'gy_2'}, use_global_device_ids=true, to_apply=%region_4.0 | all-reduce | flops 1 | bytes 8 | tf_op jit(solution)/shard_map/psum | solution.py:31
  56.8 747.0 %while.56 = (s32[]{:T(128)}, f32[16,64,256]{2,1,0:T(8,128)S(1)}, f32[16,15]{0,1:T(8,128)S(1)}, f32[64,256]{1,0:T(8,128)S(1)}, f32[64,256]{1,0:T(8,128)S(1)}, /*i...) while((s32[]{:T(128)}, f32[16,64,256]{2,1,0:T(8,128)S(1)}, ...), condition=%wide.region_16.0_spmd.clone, body=%wide.region_5.16_spmd.clone.sunk | while | flops 7373337 | bytes 4410527 | solution.py:135
  115.5 7.2 collective-permute-done.3
  165.6 7.2 collective-permute-done.3
  193.3 6.8 all-reduce.12
  215.6 7.2 collective-permute-done.3
  243.3 6.8 all-reduce.12
  265.7 7.2 collective-permute-done.3
  293.4 6.8 all-reduce.12
  315.7 7.2 collective-permute-done.3
  343.4 6.8 all-reduce.12
  365.8 7.2 collective-permute-done.3
  415.8 7.2 collective-permute-done.3
  465.9 7.2 collective-permute-done.3
  515.9 7.2 collective-permute-done.3
  566.0 7.2 collective-permute-done.3
  616.0 7.2 collective-permute-done.3
  666.1 7.2 collective-permute-done.3
  716.1 7.2 collective-permute-done.3
  766.2 7.2 collective-permute-done.3
  804.5 162.3 %while.54 = (s32[]{:T(128)}, f32[16,15]{1,0:T(8,128)S(1)}, f32[16]{0:T(128)S(1)}, s32[]{:T(128)}, s32[2]{0:T(128)S(1)}, /*index=5*/s32[1]{0:T(128)}, s32[]{:T(128)}, s32[]{:T(128)}, s32[]{:T(128)}, s32[]{:T(128)}) while((s32[]{:T(128)}, f32[16,15]{1,0:T(8,128)S(1)}, f32[16]{0:T(128)S(1)}, s32[]{:T(128)}, s32[2]{0:T(128)S(1)}, ...), condition=%wide.region_20.21_spmd, body=%wide.region_17.20_spmd.sunk | while | flops 165 | bytes 5167 | solution.py:90
  966.8 59.4 %while.55 = (s32[]{:T(128)}, f32[15]{0:T(128)S(1)}, f32[16]{0:T(128)S(1)}, f32[16,15]{1,0:T(8,128)S(1)}, s32[]{:T(128)}, /*index=5*/s32[]{:T(128)}, s32[]{:T(128)}, s32[]{:T(128)}, s32[]{:T(128)}) while((s32[]{:T(128)}, f32[15]{0:T(128)S(1)}, f32[16]{0:T(128)S(1)}, f32[16,15]{1,0:T(8,128)S(1)}, s32[]{:T(128)}, /*index=5*/s32[]{:T(128)}, ...), condition=%wide.region_23.24_spmd, body=%wide.region_21.23_spmd.sunk | while | flops 43 | bytes 490 | solution.py:97
  (634 shorter events, 723.2 us)
Async XLA Ops:
  1.4 11.7 %collective-permute-start.8 = (f32[2,2,256]{2,1,0:T(2,128)S(1)}, f32[2,2,256]{2,1,0:T(2,128)S(1)}, u32[]{:S(2)}, u32[]{:S(2)}) collective-permute-start(f32[2,2,256]{2,1,0:T(2,128)S(1)} %get-tuple-element.581), channel_id=1, source_target_pairs={{0,64},{64,0},{1,65},{65,1},{2,66},{66,2},{3,67},{67,3},{4,68},{68... | collective-permute-start | bytes 12296 | tf_op jit(solution)/shard_map/ppermute | solution.py:20
  2.8 10.4 %collective-permute-start.9 = (f32[2,2,256]{2,1,0:T(2,128)S(1)}, f32[2,2,256]{2,1,0:T(2,128)S(1)}, u32[]{:S(2)}, u32[]{:S(2)}) collective-permute-start(f32[2,2,256]{2,1,0:T(2,128)S(1)} %get-tuple-element.582), channel_id=1, source_target_pairs={{64,0},{0,64},{65,1},{1,65},{66,2},{2,66},{67,3},{3,67},{68,4},{4,... | collective-permute-start | bytes 12296 | tf_op jit(solution)/shard_map/ppermute | solution.py:22
  4.6 15.7 %collective-permute-start.6 = (f32[68,2]{1,0:T(8,128)S(1)}, f32[68,2]{1,0:T(8,128)S(1)}, u32[]{:S(2)}, u32[]{:S(2)}) collective-permute-start(f32[68,2]{1,0:T(8,128)S(1)} %get-tuple-element.584), channel_id=1, source_target_pairs={{1,0},{2,1},{3,2},{4,3},{5,4},{6,5},{7,6},{8,7},{9,8},{10,9},{11,1... | collective-permute-start | bytes 1640 | tf_op jit(solution)/shard_map/ppermute | solution.py:22
  13.1 8.2 collective-permute-start.7
  13.3 9.4 collective-permute-start.10
  13.4 9.4 collective-permute-start.11
  64.6 8.3 collective-permute-start.3
  114.5 8.2 collective-permute-start.3
  164.5 8.2 collective-permute-start.3
  214.6 8.2 collective-permute-start.3
  264.6 8.2 collective-permute-start.3
  303.4 7.3 collective-permute-start
  314.7 8.2 collective-permute-start.3
  353.4 7.3 collective-permute-start
  364.7 8.2 collective-permute-start.3
  403.5 7.3 collective-permute-start
  414.8 8.2 collective-permute-start.3
  464.8 8.2 collective-permute-start.3
  514.9 8.2 collective-permute-start.3
  564.9 8.2 collective-permute-start.3
  615.0 8.2 collective-permute-start.3
  665.0 8.2 collective-permute-start.3
  715.1 8.2 collective-permute-start.3
  765.1 8.2 collective-permute-start.3
  (50 other events, 196.7 us)
where the time goes:
time: 1040 us; the launch traced here: 1030 us
  blocking collectives  398 us (38%)
  starting transfers between devices  167 us (16%)
  loops' own time  149 us (14%)
  waiting for transfers between devices  141 us (14%)
  other arithmetic  84.3 us (8%)
  matrix products  46.7 us (4%)
  local copies, waits for them, and re-layouts  42.3 us (4%)
    psum x64, blocking collectives, one_axis_at_a_time(): x = lax.psum(x, axis)  398 us
    ppermute x34, starting transfers between devices, padded_2(): lax.ppermute(head, axis, [((i + 1) % count, i) for i in range(ends)])  163 us
    ppermute x34, waiting for transfers between devices, padded_2(): lax.ppermute(tail, axis, [(i, (i + 1) % count) for i in range(ends)])  114 us
    another operation x1, loops' own time, least_squares(): lax.fori_loop(0, columns_total, rotate, (hessenberg, target))  97.8 us
    another operation x46, other arithmetic  30.6 us
    another operation x1, loops' own time, least_squares(): lax.fori_loop(0, columns_total, substitute, jnp.zeros((columns_total,), j...  30.2 us
    ppermute x34, waiting for transfers between devices, padded_2(): lax.ppermute(head, axis, [((i + 1) % count, i) for i in range(ends)])  27.7 us
    dot_general x15, matrix products, arnoldi(): jnp.einsum('kxy,xy->k', basis, applied, precision=lax.Precision.HIGHEST)  26.6 us
  transfers between devices with their start and end apart: 68, of which 64 were waited for; matrix products, arithmetic and copies ran while one was open for 0% of the time, Pallas kernels for 0%

commit v1 on v0

v1 whole, which is shorter than its diff:
```python
import functools

import jax
import jax.numpy as jnp
from jax import lax
from jax.experimental import pallas as pl
from jax.experimental.pallas import tpu as pltpu
from jax.sharding import Mesh
from jax.sharding import PartitionSpec as P

RESTART = 15
GY = ("gy_0", "gy_1", "gy_2")
ALL = ("gx",) + GY
FIELDS = 5
ROWS, COLS, LANES, HALO = 64, 256, 128, 32
FULL = 2 * ROWS
CENTRE, SPREAD, SHRINK = 5.8, 5.0, 0.9
SCALE = 2.0 * SHRINK / SPREAD
ALPHA = SCALE * CENTRE
SQUARE = SHRINK * SHRINK


def lane_group():
    return lax.broadcasted_iota(jnp.int32, (1, LANES), 1) // HALO


def packed_edges(tiles, lane):
    group = lane_group()
    top, bottom = None, None
    for q in range(4):
        shift = (HALO * q - lane) % LANES
        moved = pltpu.roll(tiles[q], shift, 1) if shift else tiles[q]
        part = tiles[4][16 * q : 16 * q + 16]
        part = pltpu.roll(part, shift, 1) if shift else part
        top = moved if q == 0 else jnp.where(group == q, moved, top)
        bottom = part if q == 0 else jnp.where(group == q, part, bottom)
    return top, bottom


def unpacked_edges(ref, base, lane):
    top = ref[base : base + ROWS, :]
    bottom = ref[base + ROWS : base + ROWS + 16, :]
    tiles, parts = [], []
    for q in range(4):
        shift = (lane - HALO * q) % LANES
        tiles.append(pltpu.roll(top, shift, 1) if shift else top)
        parts.append(pltpu.roll(bottom, shift, 1) if shift else bottom)
    return tiles + [jnp.concatenate(parts, axis=0)]


def pack_body(core_ref, *refs):
    fields, (partner_ref, cross_ref, same_ref) = refs[:FIELDS], refs[FIELDS:]

    def put(ref, base, edges):
        ref[base : base + ROWS, :] = edges[0]
        ref[base + ROWS : base + ROWS + 16, :] = edges[1]

    for core in (0, 1):

        @pl.when(core_ref[0] == core)
        def _():
            left = [f[:, :LANES] for f in fields]
            right = [f[:, LANES:] for f in fields]
            give, keep = (right, left) if core == 0 else (left, right)
            for a in range(FIELDS):
                partner_ref[ROWS * a : ROWS * (a + 1), :] = give[a]
            put(partner_ref, FIELDS * ROWS, packed_edges(keep, 96 if core == 0 else 0))
            left_edge, right_edge = packed_edges(left, 0), packed_edges(right, 96)
            put(cross_ref, 0, left_edge if core == 0 else right_edge)
            put(same_ref, 0, right_edge if core == 0 else left_edge)


def basis_body(core_ref, *refs):
    fields = refs[:FIELDS]
    partner_ref, cross_ref, same_ref, own_ref, give_ref, gram_ref = refs[FIELDS : FIELDS + 6]
    data, coef, basis, image, pairs = refs[FIELDS + 6 :]
    lane = lax.broadcasted_iota(jnp.int32, (1, LANES), 1)

    for core in (0, 1):

        @pl.when(core_ref[0] == core)
        def _():
            mine, beside = (slice(0, LANES), slice(LANES, COLS))
            if core:
                mine, beside = beside, mine
            far = 96 if core == 0 else 0
            near = 96 - far
            same = unpacked_edges(same_ref, 0, far)
            cross = unpacked_edges(cross_ref, 0, far)
            inner = unpacked_edges(partner_ref, FIELDS * ROWS, near)
            for a in range(FIELDS):
                data[a, 8 : 8 + ROWS, :LANES] = fields[a][:, mine]
                data[a, 8 + ROWS : 8 + FULL, :LANES] = partner_ref[ROWS * a : ROWS * (a + 1), :]
                for row, here, there in ((8, fields[a][:, beside], same[a]), (8 + ROWS, inner[a], cross[a])):
                    low, high = (here, there) if core == 0 else (there, here)
                    tile = jnp.where(lane < HALO, low, jnp.where(lane >= LANES - HALO, high, 0.0))
                    data[a, row : row + ROWS, LANES:] = tile

    for a in range(FIELDS):
        data[a, 0:8, :] = data[a, FULL : FULL + 8, :]
        data[a, 8 + FULL : 16 + FULL, :] = data[a, 8:16, :]

    for r in range(0, FULL, 16):
        rows = slice(r, r + 16)
        at = lambda a, o: data[a, 8 + r + o : 24 + r + o, :]
        coef[0, rows, :] = SCALE * (at(2, 0) + (5.0 - CENTRE))
        vx, vy = at(3, 0), at(4, 0)
        for o in (1, 2):
            base = SCALE * (-4.0 / 3.0 if o == 1 else 1.0 / 12.0)
            turn = SCALE * (1.0 / 3.0 if o == 1 else -1.0 / 24.0)
            coef[4 * o - 3, rows, :] = base + turn * (vx + at(3, o))
            coef[4 * o - 2, rows, :] = base - turn * (vx + at(3, -o))
            coef[4 * o - 1, rows, :] = base + turn * (vy + pltpu.roll(vy, COLS - o, 1))
            coef[4 * o, rows, :] = base - turn * (vy + pltpu.roll(vy, o, 1))

    def stencil(load, r):
        rows = slice(r, r + 16)
        field = load(0)
        total = coef[0, rows, :] * field
        for o in (1, 2):
            total += coef[4 * o - 3, rows, :] * load(o)
            total += coef[4 * o - 2, rows, :] * load(-o)
            total += coef[4 * o - 1, rows, :] * pltpu.roll(field, COLS - o, 1)
            total += coef[4 * o, rows, :] * pltpu.roll(field, o, 1)
        return field, total

    def wrap(index):
        basis[index, 0:8, :] = basis[index, FULL : FULL + 8, :]
        basis[index, 8 + FULL : 16 + FULL, :] = basis[index, 8:16, :]

    basis[0, 8 : 8 + FULL, :] = jnp.zeros((FULL, COLS), jnp.float32)
    for r in range(0, FULL, 16):
        field, total = stencil(lambda o: data[1, 8 + r + o : 24 + r + o, :], r)
        start = data[0, 8 + r : 24 + r, :] - ((1.0 / SCALE) * total + CENTRE * field)
        basis[1, 8 + r : 24 + r, :] = start
        image[RESTART, r : r + 16, :] = start[:, :LANES]
    wrap(1)

    def step(j, carried):
        for r in range(0, FULL, 16):
            field, total = stencil(lambda o: basis[j + 1, 8 + r + o : 24 + r + o, :], r)
            image[j, r : r + 16, :] = total[:, :LANES] + ALPHA * field[:, :LANES]
            basis[j + 2, 8 + r : 24 + r, :] = total - SQUARE * basis[j, 8 + r : 24 + r, :]
        wrap(j + 2)
        return carried

    lax.fori_loop(0, RESTART, step, 0)
    own_ref[...] = basis[1:, 8 : 8 + ROWS, :LANES]
    give_ref[...] = basis[1:, 8 + ROWS : 8 + FULL, :LANES]

    for low in range(0, 16, 4):
        for high in range(low, 16, 4):

            def accumulate(t, sums):
                rows = pl.ds(pl.multiple_of(8 * t, 8), 8)
                first = [image[low + i, rows, :] for i in range(4)]
                second = first if low == high else [image[high + i, rows, :] for i in range(4)]
                return tuple(sums[4 * i + k] + first[i] * second[k] for i in range(4) for k in range(4))

            sums = lax.fori_loop(
                0, FULL // 8, accumulate, tuple(jnp.zeros((8, LANES), jnp.float32) for _ in range(16)), unroll=2
            )
            for i in range(4):
                for k in range(4):
                    row = jnp.sum(sums[4 * i + k], axis=0, keepdims=True)
                    at = 16 * (low + i) + high + k
                    pairs[at : at + 1, :] = row
                    if low != high:
                        at = 16 * (high + k) + low + i
                        pairs[at : at + 1, :] = row
    total = lax.dot_general(
        jnp.ones((8, LANES), jnp.float32),
        pairs[...],
        (((1,), (1,)), ((), ())),
        precision=lax.Precision.HIGHEST,
        preferred_element_type=jnp.float32,
    )
    gram_ref[...] = total


def finish_body(core_ref, sums_ref, partner_sums_ref, own_ref, got_ref, initial_ref, solution_ref, residual_ref):
    total = jnp.sum(sums_ref[...] + partner_sums_ref[...], axis=0)
    total = jnp.concatenate([total[0:1], total[1:2]], axis=1)
    lane = lax.broadcasted_iota(jnp.int32, (16, COLS), 1)
    sub = lax.broadcasted_iota(jnp.int32, (16, COLS), 0)
    spread = jnp.where(lane // 16 == sub, total, 0.0)
    pick_row = lax.broadcasted_iota(jnp.int32, (COLS, LANES), 0) % 16
    pick_col = lax.broadcasted_iota(jnp.int32, (COLS, LANES), 1)
    pick = jnp.where(pick_row == pick_col, 1.0, 0.0)
    gram = jnp.dot(spread, pick, precision=lax.Precision.HIGHEST, preferred_element_type=jnp.float32)
    columns = [jnp.broadcast_to(gram[:, k : k + 1], (16, LANES)) for k in range(16)]
    row_at = lax.broadcasted_iota(jnp.int32, (16, LANES), 0)
    for k in range(RESTART):
        inverse = 1.0 / columns[k][k : k + 1, :]
        for j in range(k + 1, 16):
            top = columns[j][k : k + 1, :] * inverse
            columns[j] = jnp.where(row_at == k, top, columns[j] - columns[k] * top)
    z = [columns[RESTART][k : k + 1, :] for k in range(RESTART)]
    left = []
    for k in range(16):
        value = 1.0 if k == 0 else 0.0
        if k > 0:
            value = value - z[k - 1]
        if k < RESTART:
            value = value - ALPHA * z[k]
        if k + 1 < RESTART:
            value = value - SQUARE * z[k + 1]
        left.append(value)
    step = [SCALE * z[k] for k in range(RESTART)]
    first = core_ref[0] == 0
    for r in range(0, ROWS, 8):
        rows = slice(r, r + 8)
        sums = []
        for ref in (own_ref, got_ref):
            change, rest = None, None
            for k in range(16):
                vector = ref[k, rows, :]
                rest = left[k] * vector if k == 0 else rest + left[k] * vector
                if k < RESTART:
                    change = step[k] * vector if k == 0 else change + step[k] * vector
            sums.append((change, rest))
        (own_change, own_rest), (got_change, got_rest) = sums
        solution_ref[rows, :LANES] = initial_ref[rows, :LANES] + jnp.where(first, own_change, got_change)
        solution_ref[rows, LANES:] = initial_ref[rows, LANES:] + jnp.where(first, got_change, own_change)
        residual_ref[rows, :LANES] = jnp.where(first, own_rest, got_rest)
        residual_ref[rows, LANES:] = jnp.where(first, got_rest, own_rest)


def call(body, out_shape, n_in, scratch=(), name=None):
    vmem = pl.BlockSpec(memory_space=pltpu.VMEM)
    return pl.pallas_call(
        body,
        out_shape=out_shape,
        in_specs=[pl.BlockSpec(memory_space=pltpu.SMEM)] + [vmem] * n_in,
        out_specs=jax.tree.map(lambda _: vmem, out_shape),
        scratch_shapes=scratch,
        name=name,
    )


def f32(*shape):
    return jax.ShapeDtypeStruct(shape, jnp.float32)


def per_device(right_side, initial, reaction, velocity_x, velocity_y):
    fields = (right_side, initial, reaction, velocity_x, velocity_y)
    core = lax.axis_index("gx").astype(jnp.int32).reshape(1)
    count = lax.axis_size(GY)
    swap = [(0, 1), (1, 0)]
    ahead = lambda g: (g + 1) % count
    behind = lambda g: (g - 1) % count
    cross = [(g, count + behind(g)) for g in range(count)] + [(count + g, ahead(g)) for g in range(count)]
    same = [(g, ahead(g)) for g in range(count)] + [(count + g, count + behind(g)) for g in range(count)]

    edge = f32(ROWS + 16, LANES)
    to_partner, to_cross, to_same = call(
        pack_body, (f32(FIELDS * ROWS + ROWS + 16, LANES), edge, edge), FIELDS, name="pack"
    )(core, *fields)
    from_partner = lax.ppermute(to_partner, "gx", swap)
    from_cross = lax.ppermute(to_cross, ALL, cross)
    from_same = lax.ppermute(to_same, ALL, same)
    own, give, gram = call(
        basis_body,
        (f32(16, ROWS, LANES), f32(16, ROWS, LANES), f32(8, COLS)),
        FIELDS + 3,
        scratch=[
            pltpu.VMEM((FIELDS, FULL + 16, COLS), jnp.float32),
            pltpu.VMEM((9, FULL, COLS), jnp.float32),
            pltpu.VMEM((RESTART + 2, FULL + 16, COLS), jnp.float32),
            pltpu.VMEM((16, FULL, LANES), jnp.float32),
            pltpu.VMEM((COLS, LANES), jnp.float32),
        ],
        name="basis",
    )(core, *fields, from_partner, from_cross, from_same)
    got = lax.ppermute(give, "gx", swap)
    gram = gram[0].reshape(1, 2, LANES)
    sums = lax.all_to_all(jnp.broadcast_to(gram, (count, 2, LANES)), GY, 0, 0, tiled=True)
    partner_sums = lax.ppermute(sums, "gx", swap)
    return call(finish_body, (f32(ROWS, COLS), f32(ROWS, COLS)), 5, name="finish")(
        core, sums, partner_sums, own, got, initial
    )


def solution(mesh):
    torus = Mesh(mesh.devices.reshape(mesh.shape["gx"], 4, 4, 4), ALL)
    placed = P("gx", GY)
    return jax.shard_map(
        per_device,
        mesh=torus,
        in_specs=(placed,) * FIELDS,
        out_specs=(placed, placed),
        check_vma=False,
    )
```

time: 1040 us -> 49.5 us (0.05)
  blocking collectives: 398 us -> 12.7 us
  loops' own time: 149 us -> 0 us
  starting transfers between devices: 167 us -> 19.5 us
  waiting for transfers between devices: 141 us -> 2.22 us
  other arithmetic: 84.3 us -> 0 us
  matrix products: 46.7 us -> 0 us
  local copies, waits for them, and re-layouts: 42.3 us -> 2.82 us
  Pallas kernels: 0 us -> 11.4 us
    psum x64 -> x0, blocking collectives: 398 us -> none  [one_axis_at_a_time(): x = lax.psum(x, axis)]
    another operation x3 -> x0, loops' own time: 149 us -> none  [the longest x1 97.8 us: least_squares(): lax.fori_loop(0, columns_total, rotate, (hessenberg, target))]
    ppermute x68 -> x5, starting transfers between devices: 167 us -> 19.5 us  [the longest x1 8.72 us: per_device(): got = lax.ppermute(give, 'gx', swap)]
    ppermute x68 -> x5, waiting for transfers between devices: 141 us -> 2.22 us  [the longest x1 1.31 us: per_device(): from_same = lax.ppermute(to_same, ALL, same)]
    dot_general x33 -> x0, matrix products: 46.7 us -> none  [the longest x15 26.6 us: arnoldi(): jnp.einsum('kxy,xy->k', basis, applied, precision=lax.Precision.HIGHEST)]
    dynamic_slice x60 -> x0, local copies, waits for them, and re-layouts: 36.8 us -> none  [the longest x15 9.87 us: rotate(): diagonal_entry = top_row[column]]
    reduce_sum x46 -> x0, other arithmetic: 32.2 us -> none  [the longest x15 12.9 us: arnoldi(): jnp.sum(applied * applied)]
    another operation x46 -> x0, other arithmetic: 30.6 us -> none
  transfers between devices with their start and end apart: 68 -> 5, of which waited for: 64 -> 2; matrix products, arithmetic and copies ran while one was open for 0% -> 1% of each run, Pallas kernels for 0% -> 0%
where the time goes in v1:
time: 49.5 us; the launch traced here: 49.2 us
  starting transfers between devices  19.5 us (39%)
  blocking collectives  12.7 us (26%)
  Pallas kernels  11.4 us (23%)
  local copies, waits for them, and re-layouts  2.82 us (6%)
  waiting for transfers between devices  2.22 us (4%)
  between operations  0.65 us (1%)
    all_to_all x1, blocking collectives, per_device(): lax.all_to_all(jnp.broadcast_to(gram, (count, 2, LANES)), GY, 0, 0, tiled...  12.7 us
    ppermute x1, starting transfers between devices, per_device(): got = lax.ppermute(give, 'gx', swap)  8.72 us
    ppermute x1, starting transfers between devices, per_device(): from_same = lax.ppermute(to_same, ALL, same)  7.31 us
    pallas_call x1, Pallas kernels, per_device(): call(basis_body, (f32(16, ROWS, LANES), f32(16, ROWS, LANES), f32(8, COLS...  7.01 us
    pallas_call x1, Pallas kernels, per_device(): call(finish_body, (f32(ROWS, COLS), f32(ROWS, COLS)), 5, name='finish')  2.53 us
    unnamed x12, local copies, waits for them, and re-layouts  2.1 us
    pallas_call x1, Pallas kernels, per_device(): call(pack_body, (f32(FIELDS * ROWS + ROWS + 16, LANES), edge, edge), FIEL...  1.83 us
    ppermute x1, starting transfers between devices, per_device(): from_partner = lax.ppermute(to_partner, 'gx', swap)  1.36 us
  transfers between devices with their start and end apart: 5, of which 2 were waited for; matrix products, arithmetic and copies ran while one was open for 1% of the time, Pallas kernels for 0%

profile of v1, /device:TPU:1, one launch (start us, length us, event | category | flops | bytes accessed | tf_op | source)
XLA Modules:
  0.0 49.2 jit_solution(18217190158185135098)
XLA Ops:
  0.6 1.8 %pack.1 = (f32[400,128]{1,0:T(8,128)}, f32[80,128]{1,0:T(8,128)}, f32[80,128]{1,0:T(8,128)}) custom-call(s32[1]{0:T(128)} %bitcast.core_ref, f32[64,256]{1,0:T(8,128)} %refs_0_.3, f32[64,256]{1,0:T(8,128)} %initial_ref.1, f32[64,256]{1,0:T(8,128)} %refs_2_.3, f32[64,256]{1,0:T(8,128)} %refs_3_.3, f32[64,256]{1,0:T(8,128)} %refs_4_.3), custom_call_target="tpu_custom_call" | custom-call | tf_op jit(solution)/shard_map/pack/pallas_call | solution.py:256
  2.5 1.4 %collective-permute-start = (f32[400,128]{1,0:T(8,128)}, f32[400,128]{1,0:T(8,128)S(1)}, u32[]{:S(2)}, u32[]{:S(2)}) collective-permute-start(f32[400,128]{1,0:T(8,128)} %get-tuple-element.8), channel_id=1, source_target_pairs={{0,64},{64,0},{1,65},{65,1},{2,66},{66,2},{3,67},{67,3},{4,68},{68... | collective-permute-start | bytes 614408 | tf_op jit(solution)/shard_map/ppermute | solution.py:259
  3.8 1.2 %collective-permute-start.1 = (f32[80,128]{1,0:T(8,128)}, f32[80,128]{1,0:T(8,128)S(1)}, u32[]{:S(2)}, u32[]{:S(2)}) collective-permute-start(f32[80,128]{1,0:T(8,128)} %get-tuple-element.9), channel_id=1, source_target_pairs={{0,127},{1,64},{2,65},{3,66},{4,67},{5,68},{6,69},{7,70},{8,71},{9... | collective-permute-start | bytes 122888 | tf_op jit(solution)/shard_map/ppermute | solution.py:260
  5.1 7.3 %collective-permute-start.2 = (f32[80,128]{1,0:T(8,128)}, f32[80,128]{1,0:T(8,128)S(1)}, u32[]{:S(2)}, u32[]{:S(2)}) collective-permute-start(f32[80,128]{1,0:T(8,128)} %get-tuple-element.10), channel_id=1, source_target_pairs={{0,1},{1,2},{2,3},{3,4},{4,5},{5,6},{6,7},{7,8},{8,9},{9,10},{10,1... | collective-permute-start | bytes 122888 | tf_op jit(solution)/shard_map/ppermute | solution.py:261
  12.4 0.0 collective-permute-done.1.refs_6_
  12.4 0.0 copy-start.4
  12.4 1.3 %collective-permute-done.2.refs_7_ = f32[80,128]{1,0:T(8,128)S(1)} collective-permute-done((f32[80,128]{1,0:T(8,128)}, f32[80,128]{1,0:T(8,128)S(1)}, u32[]{:S(2)}, u32[]{:S(2)}) %collective-permute-start.2) | collective-permute-done | bytes 40992 | tf_op jit(solution)/shard_map/ppermute | solution.py:261
  13.7 0.0 copy-start.5
  13.7 0.0 collective-permute-done.refs_5_
  13.7 0.0 copy-done.4
  13.7 0.6 %copy-done.5 = f32[80,128]{1,0:T(8,128)} copy-done((f32[80,128]{1,0:T(8,128)}, f32[80,128]{1,0:T(8,128)S(1)}, u32[]{:S(2)}) %copy-start.5) | copy-done | bytes 40984
  14.3 0.0 copy-start.2
  14.3 0.7 %copy-done.2 = f32[400,128]{1,0:T(8,128)} copy-done((f32[400,128]{1,0:T(8,128)}, f32[400,128]{1,0:T(8,128)S(1)}, u32[]{:S(2)}) %copy-start.2) | copy-done | bytes 204824
  15.0 7.0 %basis.1 = (f32[16,64,128]{2,1,0:T(8,128)}, f32[16,64,128]{2,1,0:T(8,128)}, f32[8,256]{1,0:T(8,128)}) custom-call(s32[1]{0:T(128)} %bitcast.core_ref, f32[64,256]{1,0:T(8,128)} %refs_0_.3, f32[64,256]{1,0:T(8,128)} %initial_ref.1, f32[64,256]{1,0:T(8,128)} %refs_2_.3, f32[64,256]{1,0:T(8,128)} %refs_3_.3, f32[64,256]{1,0:T(8,128)} %refs_4_.3, ...), custom_call_target="tpu_custom_call" | custom-call | tf_op jit(solution)/shard_map/basis/pallas_call | solution.py:262
  22.0 8.7 %collective-permute-start.4 = (f32[16,64,128]{2,1,0:T(8,128)}, f32[16,64,128]{2,1,0:T(8,128)S(1)}, u32[]{:S(2)}, u32[]{:S(2)}) collective-permute-start(f32[16,64,128]{2,1,0:T(8,128)} %get-tuple-element.13), channel_id=1, source_target_pairs={{0,64},{64,0},{1,65},{65,1},{2,66},{66,2},{3,67},{67,3},{4,68},{68... | collective-permute-start | bytes 1572872 | tf_op jit(solution)/shard_map/ppermute | solution.py:275
  30.7 0.7 %slice.3 = f32[1,256]{1,0:T(1,128)S(1)} slice(f32[8,256]{1,0:T(8,128)} %get-tuple-element.11), slice={[0:1], [0:256]} | slice | bytes 2048 | tf_op jit(solution)/shard_map/slice | solution.py:276
  31.5 12.7 %all_to_all.5.sums_ref = f32[64,2,128]{2,1,0:T(2,128)S(1)} all-to-all(f32[64,2,128]{2,1,0:T(2,128)S(1)} %broadcast_in_dim.8), channel_id=1, replica_groups=mesh['gx'=2,'gy_0'=4,'gy_1'=4,'gy_2'=4] {'gy_0','gy_1','gy_2'}, dimensions={0} | all-to-all | bytes 131072 | tf_op jit(solution)/shard_map/all_to_all | solution.py:277
  44.1 0.8 %collective-permute-start.3 = (f32[64,2,128]{2,1,0:T(2,128)S(1)}, f32[64,2,128]{2,1,0:T(2,128)S(1)}, u32[]{:S(2)}, u32[]{:S(2)}) collective-permute-start(f32[64,2,128]{2,1,0:T(2,128)S(1)} %all_to_all.5.sums_ref), channel_id=1, source_target_pairs={{0,64},{64,0},{1,65},{65,1},{2,66},{66,2},{3,67},{67,3},{4,68},{68... | collective-permute-start | bytes 196616 | tf_op jit(solution)/shard_map/ppermute | solution.py:278
  45.0 0.9 %collective-permute-done.3.partner_sums_ref = f32[64,2,128]{2,1,0:T(2,128)S(1)} collective-permute-done((f32[64,2,128]{2,1,0:T(2,128)S(1)}, f32[64,2,128]{2,1,0:T(2,128)S(1)}, u32[]{:S(2)}, u32[]{:S(2)}) %collective-permute-start.3) | collective-permute-done | bytes 65568 | tf_op jit(solution)/shard_map/ppermute | solution.py:278
  45.9 0.0 collective-permute-done.4.got_ref
  45.9 0.0 copy-done.1
  45.9 0.6 %copy-done.3 = f32[64,2,128]{2,1,0:T(2,128)} copy-done((f32[64,2,128]{2,1,0:T(2,128)}, f32[64,2,128]{2,1,0:T(2,128)S(1)}, u32[]{:S(2)}) %copy-start.3) | copy-done | bytes 65560
  46.5 0.2 copy-done
  46.7 2.5 %finish.1 = (f32[64,256]{1,0:T(8,128)}, f32[64,256]{1,0:T(8,128)}) custom-call(s32[1]{0:T(128)} %bitcast.core_ref, f32[64,2,128]{2,1,0:T(2,128)} %copy-done.1, f32[64,2,128]{2,1,0:T(2,128)} %copy-done.3, f32[16,64,128]{2,1,0:T(8,128)} %get-tuple-element.12.own_ref, f32[16,64,128]{2,1,0:T(8,128)} %copy-done, f32[64,256]{1,0:T(8,128)} %initial_ref.1), custom_call_target="tpu_custom_call" | custom-call | tf_op jit(solution)/shard_map/finish/pallas_call | solution.py:279
  (4 shorter events, 0.0 us)
Async XLA Ops:
  2.5 11.2 %collective-permute-start = (f32[400,128]{1,0:T(8,128)}, f32[400,128]{1,0:T(8,128)S(1)}, u32[]{:S(2)}, u32[]{:S(2)}) collective-permute-start(f32[400,128]{1,0:T(8,128)} %get-tuple-element.8), channel_id=1, source_target_pairs={{0,64},{64,0},{1,65},{65,1},{2,66},{66,2},{3,67},{67,3},{4,68},{68... | collective-permute-start | bytes 614408 | tf_op jit(solution)/shard_map/ppermute | solution.py:259
  3.8 8.6 %collective-permute-start.1 = (f32[80,128]{1,0:T(8,128)}, f32[80,128]{1,0:T(8,128)S(1)}, u32[]{:S(2)}, u32[]{:S(2)}) collective-permute-start(f32[80,128]{1,0:T(8,128)} %get-tuple-element.9), channel_id=1, source_target_pairs={{0,127},{1,64},{2,65},{3,66},{4,67},{5,68},{6,69},{7,70},{8,71},{9... | collective-permute-start | bytes 122888 | tf_op jit(solution)/shard_map/ppermute | solution.py:260
  5.1 8.6 %collective-permute-start.2 = (f32[80,128]{1,0:T(8,128)}, f32[80,128]{1,0:T(8,128)S(1)}, u32[]{:S(2)}, u32[]{:S(2)}) collective-permute-start(f32[80,128]{1,0:T(8,128)} %get-tuple-element.10), channel_id=1, source_target_pairs={{0,1},{1,2},{2,3},{3,4},{4,5},{5,6},{6,7},{7,8},{8,9},{9,10},{10,1... | collective-permute-start | bytes 122888 | tf_op jit(solution)/shard_map/ppermute | solution.py:261
  12.4 1.3 %copy-start.4 = (f32[80,128]{1,0:T(8,128)}, f32[80,128]{1,0:T(8,128)S(1)}, u32[]{:S(2)}) copy-start(f32[80,128]{1,0:T(8,128)S(1)} %collective-permute-done.1.refs_6_) | copy-start | bytes 122884
  13.7 0.6 %copy-start.5 = (f32[80,128]{1,0:T(8,128)}, f32[80,128]{1,0:T(8,128)S(1)}, u32[]{:S(2)}) copy-start(f32[80,128]{1,0:T(8,128)S(1)} %collective-permute-done.2.refs_7_) | copy-start | bytes 122884
  14.3 0.7 %copy-start.2 = (f32[400,128]{1,0:T(8,128)}, f32[400,128]{1,0:T(8,128)S(1)}, u32[]{:S(2)}) copy-start(f32[400,128]{1,0:T(8,128)S(1)} %collective-permute-done.refs_5_) | copy-start | bytes 614404
  22.0 23.9 %collective-permute-start.4 = (f32[16,64,128]{2,1,0:T(8,128)}, f32[16,64,128]{2,1,0:T(8,128)S(1)}, u32[]{:S(2)}, u32[]{:S(2)}) collective-permute-start(f32[16,64,128]{2,1,0:T(8,128)} %get-tuple-element.13), channel_id=1, source_target_pairs={{0,64},{64,0},{1,65},{65,1},{2,66},{66,2},{3,67},{67,3},{4,68},{68... | collective-permute-start | bytes 1572872 | tf_op jit(solution)/shard_map/ppermute | solution.py:275
  44.1 1.8 %copy-start.1 = (f32[64,2,128]{2,1,0:T(2,128)}, f32[64,2,128]{2,1,0:T(2,128)S(1)}, u32[]{:S(2)}) copy-start(f32[64,2,128]{2,1,0:T(2,128)S(1)} %all_to_all.5.sums_ref) | copy-start | bytes 196612
  44.1 1.8 %collective-permute-start.3 = (f32[64,2,128]{2,1,0:T(2,128)S(1)}, f32[64,2,128]{2,1,0:T(2,128)S(1)}, u32[]{:S(2)}, u32[]{:S(2)}) collective-permute-start(f32[64,2,128]{2,1,0:T(2,128)S(1)} %all_to_all.5.sums_ref), channel_id=1, source_target_pairs={{0,64},{64,0},{1,65},{65,1},{2,66},{66,2},{3,67},{67,3},{4,68},{68... | collective-permute-start | bytes 196616 | tf_op jit(solution)/shard_map/ppermute | solution.py:278
  45.9 0.6 %copy-start.3 = (f32[64,2,128]{2,1,0:T(2,128)}, f32[64,2,128]{2,1,0:T(2,128)S(1)}, u32[]{:S(2)}) copy-start(f32[64,2,128]{2,1,0:T(2,128)S(1)} %collective-permute-done.3.partner_sums_ref) | copy-start | bytes 196612
  45.9 0.8 %copy-start = (f32[16,64,128]{2,1,0:T(8,128)}, f32[16,64,128]{2,1,0:T(8,128)S(1)}, u32[]{:S(2)}) copy-start(f32[16,64,128]{2,1,0:T(8,128)S(1)} %collective-permute-done.4.got_ref) | copy-start | bytes 1572868

commit v2 on v1

--- a/solution.py
+++ b/solution.py
@@ -49,7 +49,9 @@
 
 
 def pack_body(core_ref, *refs):
-    fields, (partner_ref, cross_ref, same_ref) = refs[:FIELDS], refs[FIELDS:]
+    fields, (same_ref, cross_ref, partner_ref, held_ref) = refs[:FIELDS], refs[FIELDS:]
+    for a in range(FIELDS):
+        held_ref[a] = fields[a][...]
 
     def put(ref, base, edges):
         ref[base : base + ROWS, :] = edges[0]
@@ -71,9 +73,8 @@
 
 
 def basis_body(core_ref, *refs):
-    fields = refs[:FIELDS]
-    partner_ref, cross_ref, same_ref, own_ref, give_ref, gram_ref = refs[FIELDS : FIELDS + 6]
-    data, coef, basis, image, pairs = refs[FIELDS + 6 :]
+    held_ref, partner_ref, cross_ref, same_ref, own_ref, give_ref, gram_ref = refs[:7]
+    data, coef, basis, image, pairs = refs[7:]
     lane = lax.broadcasted_iota(jnp.int32, (1, LANES), 1)
 
     for core in (0, 1):
@@ -89,9 +90,9 @@
             cross = unpacked_edges(cross_ref, 0, far)
             inner = unpacked_edges(partner_ref, FIELDS * ROWS, near)
             for a in range(FIELDS):
-                data[a, 8 : 8 + ROWS, :LANES] = fields[a][:, mine]
+                data[a, 8 : 8 + ROWS, :LANES] = held_ref[a, :, mine]
                 data[a, 8 + ROWS : 8 + FULL, :LANES] = partner_ref[ROWS * a : ROWS * (a + 1), :]
-                for row, here, there in ((8, fields[a][:, beside], same[a]), (8 + ROWS, inner[a], cross[a])):
+                for row, here, there in ((8, held_ref[a, :, beside], same[a]), (8 + ROWS, inner[a], cross[a])):
                     low, high = (here, there) if core == 0 else (there, here)
                     tile = jnp.where(lane < HALO, low, jnp.where(lane >= LANES - HALO, high, 0.0))
                     data[a, row : row + ROWS, LANES:] = tile
@@ -175,11 +176,12 @@
         precision=lax.Precision.HIGHEST,
         preferred_element_type=jnp.float32,
     )
-    gram_ref[...] = total
-
-
-def finish_body(core_ref, sums_ref, partner_sums_ref, own_ref, got_ref, initial_ref, solution_ref, residual_ref):
-    total = jnp.sum(sums_ref[...] + partner_sums_ref[...], axis=0)
+    both = jnp.concatenate([total[0:1, :LANES], total[0:1, LANES:]], axis=0)
+    gram_ref[...] = jnp.broadcast_to(both[None], gram_ref.shape)
+
+
+def finish_body(core_ref, sums_ref, own_ref, got_ref, held_ref, solution_ref, residual_ref):
+    total = jnp.sum(sums_ref[...], axis=0)
     total = jnp.concatenate([total[0:1], total[1:2]], axis=1)
     lane = lax.broadcasted_iota(jnp.int32, (16, COLS), 1)
     sub = lax.broadcasted_iota(jnp.int32, (16, COLS), 0)
@@ -220,26 +222,32 @@
                     change = step[k] * vector if k == 0 else change + step[k] * vector
             sums.append((change, rest))
         (own_change, own_rest), (got_change, got_rest) = sums
-        solution_ref[rows, :LANES] = initial_ref[rows, :LANES] + jnp.where(first, own_change, got_change)
-        solution_ref[rows, LANES:] = initial_ref[rows, LANES:] + jnp.where(first, got_change, own_change)
+        solution_ref[rows, :LANES] = held_ref[1, rows, :LANES] + jnp.where(first, own_change, got_change)
+        solution_ref[rows, LANES:] = held_ref[1, rows, LANES:] + jnp.where(first, got_change, own_change)
         residual_ref[rows, :LANES] = jnp.where(first, own_rest, got_rest)
         residual_ref[rows, LANES:] = jnp.where(first, got_rest, own_rest)
 
 
-def call(body, out_shape, n_in, scratch=(), name=None):
+def call(body, out_shape, scratch=(), name=None, staged=True):
     vmem = pl.BlockSpec(memory_space=pltpu.VMEM)
-    return pl.pallas_call(
-        body,
-        out_shape=out_shape,
-        in_specs=[pl.BlockSpec(memory_space=pltpu.SMEM)] + [vmem] * n_in,
-        out_specs=jax.tree.map(lambda _: vmem, out_shape),
-        scratch_shapes=scratch,
-        name=name,
-    )
-
-
-def f32(*shape):
-    return jax.ShapeDtypeStruct(shape, jnp.float32)
+
+    def run(core, *args):
+        if staged:
+            args = [pltpu.with_memory_space_constraint(a, pltpu.VMEM) for a in args]
+        return pl.pallas_call(
+            body,
+            out_shape=out_shape,
+            in_specs=[pl.BlockSpec(memory_space=pltpu.SMEM)] + [vmem] * len(args),
+            out_specs=tuple(vmem for _ in out_shape),
+            scratch_shapes=scratch,
+            name=name,
+        )(core, *args)
+
+    return run
+
+
+def on_chip(*shape):
+    return pltpu.VMEM(shape, jnp.float32)
 
 
 def per_device(right_side, initial, reaction, velocity_x, velocity_y):
@@ -252,33 +260,32 @@
     cross = [(g, count + behind(g)) for g in range(count)] + [(count + g, ahead(g)) for g in range(count)]
     same = [(g, ahead(g)) for g in range(count)] + [(count + g, count + behind(g)) for g in range(count)]
 
-    edge = f32(ROWS + 16, LANES)
-    to_partner, to_cross, to_same = call(
-        pack_body, (f32(FIELDS * ROWS + ROWS + 16, LANES), edge, edge), FIELDS, name="pack"
+    edge = on_chip(ROWS + 16, LANES)
+    to_same, to_cross, to_partner, held = call(
+        pack_body,
+        (edge, edge, on_chip(FIELDS * ROWS + ROWS + 16, LANES), on_chip(FIELDS, ROWS, COLS)),
+        name="pack",
+        staged=False,
     )(core, *fields)
+    from_same = lax.ppermute(to_same, ALL, same)
+    from_cross = lax.ppermute(to_cross, ALL, cross)
     from_partner = lax.ppermute(to_partner, "gx", swap)
-    from_cross = lax.ppermute(to_cross, ALL, cross)
-    from_same = lax.ppermute(to_same, ALL, same)
     own, give, gram = call(
         basis_body,
-        (f32(16, ROWS, LANES), f32(16, ROWS, LANES), f32(8, COLS)),
-        FIELDS + 3,
+        (on_chip(16, ROWS, LANES), on_chip(16, ROWS, LANES), on_chip(2 * count, 2, LANES)),
         scratch=[
-            pltpu.VMEM((FIELDS, FULL + 16, COLS), jnp.float32),
-            pltpu.VMEM((9, FULL, COLS), jnp.float32),
-            pltpu.VMEM((RESTART + 2, FULL + 16, COLS), jnp.float32),
-            pltpu.VMEM((16, FULL, LANES), jnp.float32),
-            pltpu.VMEM((COLS, LANES), jnp.float32),
+            on_chip(FIELDS, FULL + 16, COLS),
+            on_chip(9, FULL, COLS),
+            on_chip(RESTART + 2, FULL + 16, COLS),
+            on_chip(16, FULL, LANES),
+            on_chip(COLS, LANES),
         ],
         name="basis",
-    )(core, *fields, from_partner, from_cross, from_same)
+    )(core, held, from_partner, from_cross, from_same)
     got = lax.ppermute(give, "gx", swap)
-    gram = gram[0].reshape(1, 2, LANES)
-    sums = lax.all_to_all(jnp.broadcast_to(gram, (count, 2, LANES)), GY, 0, 0, tiled=True)
-    partner_sums = lax.ppermute(sums, "gx", swap)
-    return call(finish_body, (f32(ROWS, COLS), f32(ROWS, COLS)), 5, name="finish")(
-        core, sums, partner_sums, own, got, initial
-    )
+    sums = lax.all_to_all(gram, ALL, 0, 0, tiled=True)
+    result = jax.ShapeDtypeStruct((ROWS, COLS), jnp.float32)
+    return call(finish_body, (result, result), name="finish")(core, sums, own, got, held)
 
 
 def solution(mesh):

time: 49.5 us -> 41.6 us (0.84)
  Pallas kernels: 11.4 us -> 7.73 us
  local copies, waits for them, and re-layouts: 2.82 us -> 0 us
  waiting for transfers between devices: 2.22 us -> 1.11 us
  starting transfers between devices: 19.5 us -> 18.8 us
    pallas_call x3, Pallas kernels: 11.4 us -> 7.73 us  [run(): pl.pallas_call(body, out_shape=out_shape, in_specs=[pl.BlockSpec(memory_s...]
    unnamed x12 -> x0, local copies, waits for them, and re-layouts: 2.1 us -> none
    ppermute x1 -> x0, waiting for transfers between devices: 0.9 us -> none  [per_device(): partner_sums = lax.ppermute(sums, 'gx', swap)]
    ppermute x1 -> x0, starting transfers between devices: 0.85 us -> none  [per_device(): partner_sums = lax.ppermute(sums, 'gx', swap)]
    slice x1 -> x0, local copies, waits for them, and re-layouts: 0.7 us -> none  [per_device(): gram = gram[0].reshape(1, 2, LANES)]
  transfers between devices with their start and end apart: 5 -> 4, of which waited for: 2 -> 1; matrix products, arithmetic and copies ran while one was open for 1% -> 0% of each run, Pallas kernels for 0% -> 0%
where the time goes in v2:
time: 41.6 us; the launch traced here: 41.4 us
  starting transfers between devices  18.8 us (45%)
  blocking collectives  13.1 us (31%)
  Pallas kernels  7.73 us (19%)
  waiting for transfers between devices  1.11 us (3%)
  between operations  0.66 us (2%)
    all_to_all x1, blocking collectives, per_device(): sums = lax.all_to_all(gram, ALL, 0, 0, tiled=True)  13.1 us
    ppermute x1, starting transfers between devices, per_device(): got = lax.ppermute(give, 'gx', swap)  8.8 us
    pallas_call x3, Pallas kernels, run(): pl.pallas_call(body, out_shape=out_shape, in_specs=[pl.BlockSpec(memory_s...  7.73 us
    ppermute x1, starting transfers between devices, per_device(): from_same = lax.ppermute(to_same, ALL, same)  7.22 us
    ppermute x1, starting transfers between devices, per_device(): from_partner = lax.ppermute(to_partner, 'gx', swap)  1.44 us
    ppermute x1, starting transfers between devices, per_device(): from_cross = lax.ppermute(to_cross, ALL, cross)  1.33 us
    ppermute x1, waiting for transfers between devices, per_device(): from_same = lax.ppermute(to_same, ALL, same)  1.1 us
  transfers between devices with their start and end apart: 4, of which 1 were waited for; matrix products, arithmetic and copies ran while one was open for 0% of the time, Pallas kernels for 0%

profile of v2, /device:TPU:1, one launch (start us, length us, event | category | flops | bytes accessed | tf_op | source)
XLA Modules:
  0.0 41.4 jit_solution(6555157264049433141)
XLA Ops:
  0.6 1.1 %pack.1 = (f32[80,128]{1,0:T(8,128)S(1)}, f32[80,128]{1,0:T(8,128)S(1)}, f32[400,128]{1,0:T(8,128)S(1)}, f32[5,64,256]{2,1,0:T(8,128)S(1)}) custom-call(s32[1]{0:T(128)} %bitcast.core_ref, f32[64,256]{1,0:T(8,128)} %refs_0_.1, f32[64,256]{1,0:T(8,128)} %refs_1_.1, f32[64,256]{1,0:T(8,128)} %refs_2_.1, f32[64,256]{1,0:T(8,128)} %refs_3_.1, f32[64,256]{1,0:T(8,128)} %refs_4_.1), custom_call_target="tpu_custom_call" | custom-call | tf_op jit(solution)/shard_map/pack/pallas_call | solution.py:237
  1.8 1.4 %collective-permute-start = (f32[400,128]{1,0:T(8,128)S(1)}, f32[400,128]{1,0:T(8,128)S(1)}, u32[]{:S(2)}, u32[]{:S(2)}) collective-permute-start(f32[400,128]{1,0:T(8,128)S(1)} %get-tuple-element.10), channel_id=1, source_target_pairs={{0,64},{64,0},{1,65},{65,1},{2,66},{66,2},{3,67},{67,3},{4,68},{68... | collective-permute-start | bytes 614408 | tf_op jit(solution)/shard_map/ppermute | solution.py:272
  3.2 1.3 %collective-permute-start.1 = (f32[80,128]{1,0:T(8,128)S(1)}, f32[80,128]{1,0:T(8,128)S(1)}, u32[]{:S(2)}, u32[]{:S(2)}) collective-permute-start(f32[80,128]{1,0:T(8,128)S(1)} %get-tuple-element.11), channel_id=1, source_target_pairs={{0,127},{1,64},{2,65},{3,66},{4,67},{5,68},{6,69},{7,70},{8,71},{9... | collective-permute-start | bytes 122888 | tf_op jit(solution)/shard_map/ppermute | solution.py:271
  4.6 7.2 %collective-permute-start.2 = (f32[80,128]{1,0:T(8,128)S(1)}, f32[80,128]{1,0:T(8,128)S(1)}, u32[]{:S(2)}, u32[]{:S(2)}) collective-permute-start(f32[80,128]{1,0:T(8,128)S(1)} %get-tuple-element.12), channel_id=1, source_target_pairs={{0,1},{1,2},{2,3},{3,4},{4,5},{5,6},{6,7},{7,8},{8,9},{9,10},{10,1... | collective-permute-start | bytes 122888 | tf_op jit(solution)/shard_map/ppermute | solution.py:270
  11.8 0.0 collective-permute-done.1.refs_2_
  11.8 1.1 %collective-permute-done.2.refs_3_ = f32[80,128]{1,0:T(8,128)S(1)} collective-permute-done((f32[80,128]{1,0:T(8,128)S(1)}, f32[80,128]{1,0:T(8,128)S(1)}, u32[]{:S(2)}, u32[]{:S(2)}) %collective-permute-start.2) | collective-permute-done | bytes 40992 | tf_op jit(solution)/shard_map/ppermute | solution.py:270
  12.9 0.0 collective-permute-done.refs_1_
  12.9 5.2 %basis.1 = (f32[16,64,128]{2,1,0:T(8,128)S(1)}, f32[16,64,128]{2,1,0:T(8,128)S(1)}, f32[128,2,128]{2,1,0:T(2,128)S(1)}) custom-call(s32[1]{0:T(128)} %bitcast.core_ref, f32[5,64,256]{2,1,0:T(8,128)S(1)} %get-tuple-element.9.refs_0_.held_ref, f32[400,128]{1,0:T(8,128)S(1)} %collective-permute-done.refs_1_, f32[80,128]{1,0:T(8,128)S(1)} %collective-permute-done.1.refs_2_, ...), custom_call_target="tpu_custom_call" | custom-call | tf_op jit(solution)/shard_map/basis/pallas_call | solution.py:237
  18.1 8.8 %collective-permute-start.3 = (f32[16,64,128]{2,1,0:T(8,128)S(1)}, f32[16,64,128]{2,1,0:T(8,128)S(1)}, u32[]{:S(2)}, u32[]{:S(2)}) collective-permute-start(f32[16,64,128]{2,1,0:T(8,128)S(1)} %get-tuple-element.15), channel_id=1, source_target_pairs={{0,64},{64,0},{1,65},{65,1},{2,66},{66,2},{3,67},{67,3},{4,68},{68... | collective-permute-start | bytes 1572872 | tf_op jit(solution)/shard_map/ppermute | solution.py:285
  26.9 13.1 %all_to_all.5.sums_ref = f32[128,2,128]{2,1,0:T(2,128)S(1)} all-to-all(f32[128,2,128]{2,1,0:T(2,128)S(1)} %get-tuple-element.13), channel_id=1, replica_groups=mesh['gx'=2,'gy_0'=4,'gy_1'=4,'gy_2'=4] {'gx','gy_0','gy_1','gy_2'}, dimensions={0} | all-to-all | bytes 262144 | tf_op jit(solution)/shard_map/all_to_all | solution.py:286
  40.1 0.0 collective-permute-done.3.got_ref
  40.1 1.4 %finish.1 = (f32[64,256]{1,0:T(8,128)}, f32[64,256]{1,0:T(8,128)}) custom-call(s32[1]{0:T(128)} %bitcast.core_ref, f32[128,2,128]{2,1,0:T(2,128)S(1)} %all_to_all.5.sums_ref, f32[16,64,128]{2,1,0:T(8,128)S(1)} %get-tuple-element.14.own_ref, f32[16,64,128]{2,1,0:T(8,128)S(1)} %collective-permute-done.3.got_ref, ...), custom_call_target="tpu_custom_call" | custom-call | tf_op jit(solution)/shard_map/finish/pallas_call | solution.py:237
Async XLA Ops:
  1.8 11.1 %collective-permute-start = (f32[400,128]{1,0:T(8,128)S(1)}, f32[400,128]{1,0:T(8,128)S(1)}, u32[]{:S(2)}, u32[]{:S(2)}) collective-permute-start(f32[400,128]{1,0:T(8,128)S(1)} %get-tuple-element.10), channel_id=1, source_target_pairs={{0,64},{64,0},{1,65},{65,1},{2,66},{66,2},{3,67},{67,3},{4,68},{68... | collective-permute-start | bytes 614408 | tf_op jit(solution)/shard_map/ppermute | solution.py:272
  3.2 8.6 %collective-permute-start.1 = (f32[80,128]{1,0:T(8,128)S(1)}, f32[80,128]{1,0:T(8,128)S(1)}, u32[]{:S(2)}, u32[]{:S(2)}) collective-permute-start(f32[80,128]{1,0:T(8,128)S(1)} %get-tuple-element.11), channel_id=1, source_target_pairs={{0,127},{1,64},{2,65},{3,66},{4,67},{5,68},{6,69},{7,70},{8,71},{9... | collective-permute-start | bytes 122888 | tf_op jit(solution)/shard_map/ppermute | solution.py:271
  4.6 8.3 %collective-permute-start.2 = (f32[80,128]{1,0:T(8,128)S(1)}, f32[80,128]{1,0:T(8,128)S(1)}, u32[]{:S(2)}, u32[]{:S(2)}) collective-permute-start(f32[80,128]{1,0:T(8,128)S(1)} %get-tuple-element.12), channel_id=1, source_target_pairs={{0,1},{1,2},{2,3},{3,4},{4,5},{5,6},{6,7},{7,8},{8,9},{9,10},{10,1... | collective-permute-start | bytes 122888 | tf_op jit(solution)/shard_map/ppermute | solution.py:270
  18.1 21.9 %collective-permute-start.3 = (f32[16,64,128]{2,1,0:T(8,128)S(1)}, f32[16,64,128]{2,1,0:T(8,128)S(1)}, u32[]{:S(2)}, u32[]{:S(2)}) collective-permute-start(f32[16,64,128]{2,1,0:T(8,128)S(1)} %get-tuple-element.15), channel_id=1, source_target_pairs={{0,64},{64,0},{1,65},{65,1},{2,66},{66,2},{3,67},{67,3},{4,68},{68... | collective-permute-start | bytes 1572872 | tf_op jit(solution)/shard_map/ppermute | solution.py:285

commit v3 on v2

--- a/solution.py
+++ b/solution.py
@@ -1,5 +1,3 @@
-import functools
-
 import jax
 import jax.numpy as jnp
 from jax import lax
@@ -7,6 +5,7 @@
 from jax.experimental.pallas import tpu as pltpu
 from jax.sharding import Mesh
 from jax.sharding import PartitionSpec as P
+
 
 RESTART = 15
 GY = ("gy_0", "gy_1", "gy_2")
@@ -228,7 +227,7 @@
         residual_ref[rows, LANES:] = jnp.where(first, got_rest, own_rest)
 
 
-def call(body, out_shape, scratch=(), name=None, staged=True):
+def call(body, out_shape, scratch=(), staged=True):
     vmem = pl.BlockSpec(memory_space=pltpu.VMEM)
 
     def run(core, *args):
@@ -240,7 +239,6 @@
             in_specs=[pl.BlockSpec(memory_space=pltpu.SMEM)] + [vmem] * len(args),
             out_specs=tuple(vmem for _ in out_shape),
             scratch_shapes=scratch,
-            name=name,
         )(core, *args)
 
     return run
@@ -262,10 +260,7 @@
 
     edge = on_chip(ROWS + 16, LANES)
     to_same, to_cross, to_partner, held = call(
-        pack_body,
-        (edge, edge, on_chip(FIELDS * ROWS + ROWS + 16, LANES), on_chip(FIELDS, ROWS, COLS)),
-        name="pack",
-        staged=False,
+        pack_body, (edge, edge, on_chip(FIELDS * ROWS + ROWS + 16, LANES), on_chip(FIELDS, ROWS, COLS)), staged=False
     )(core, *fields)
     from_same = lax.ppermute(to_same, ALL, same)
     from_cross = lax.ppermute(to_cross, ALL, cross)
@@ -280,12 +275,11 @@
             on_chip(16, FULL, LANES),
             on_chip(COLS, LANES),
         ],
-        name="basis",
     )(core, held, from_partner, from_cross, from_same)
     got = lax.ppermute(give, "gx", swap)
     sums = lax.all_to_all(gram, ALL, 0, 0, tiled=True)
     result = jax.ShapeDtypeStruct((ROWS, COLS), jnp.float32)
-    return call(finish_body, (result, result), name="finish")(core, sums, own, got, held)
+    return call(finish_body, (result, result))(core, sums, own, got, held)
 
 
 def solution(mesh):

time: 41.6 us -> 41.4 us (level)
  no operation moved by 1% of the time
where the time goes in v3:
time: 41.4 us; the launch traced here: 41.2 us
  starting transfers between devices  18.8 us (45%)
  blocking collectives  12.9 us (31%)
  Pallas kernels  7.73 us (19%)
  waiting for transfers between devices  1.11 us (3%)
  between operations  0.66 us (2%)
    all_to_all x1, blocking collectives, per_device(): sums = lax.all_to_all(gram, ALL, 0, 0, tiled=True)  12.9 us
    ppermute x1, starting transfers between devices, per_device(): got = lax.ppermute(give, 'gx', swap)  8.8 us
    pallas_call x3, Pallas kernels, run(): pl.pallas_call(body, out_shape=out_shape, in_specs=[pl.BlockSpec(memory_s...  7.73 us
    ppermute x1, starting transfers between devices, per_device(): from_same = lax.ppermute(to_same, ALL, same)  7.22 us
    ppermute x1, starting transfers between devices, per_device(): from_partner = lax.ppermute(to_partner, 'gx', swap)  1.47 us
    ppermute x1, starting transfers between devices, per_device(): from_cross = lax.ppermute(to_cross, ALL, cross)  1.3 us
    ppermute x1, waiting for transfers between devices, per_device(): from_same = lax.ppermute(to_same, ALL, same)  1.1 us
  transfers between devices with their start and end apart: 4, of which 1 were waited for; matrix products, arithmetic and copies ran while one was open for 0% of the time, Pallas kernels for 0%

profile of v3, /device:TPU:1, one launch (start us, length us, event | category | flops | bytes accessed | tf_op | source)
XLA Modules:
  0.0 41.2 jit_solution(6555157264049433141)
XLA Ops:
  0.6 1.1 %shard_map.68 = (f32[80,128]{1,0:T(8,128)S(1)}, f32[80,128]{1,0:T(8,128)S(1)}, f32[400,128]{1,0:T(8,128)S(1)}, f32[5,64,256]{2,1,0:T(8,128)S(1)}) custom-call(s32[1]{0:T(128)} %bitcast.core_ref, f32[64,256]{1,0:T(8,128)} %refs_0_.1, f32[64,256]{1,0:T(8,128)} %refs_1_.1, f32[64,256]{1,0:T(8,128)} %refs_2_.1, f32[64,256]{1,0:T(8,128)} %refs_3_.1, ...), custom_call_target="tpu_custom_call" | custom-call | tf_op jit(solution)/shard_map/pallas_call | solution.py:236
  1.8 1.5 %collective-permute-start = (f32[400,128]{1,0:T(8,128)S(1)}, f32[400,128]{1,0:T(8,128)S(1)}, u32[]{:S(2)}, u32[]{:S(2)}) collective-permute-start(f32[400,128]{1,0:T(8,128)S(1)} %get-tuple-element.10), channel_id=1, source_target_pairs={{0,64},{64,0},{1,65},{65,1},{2,66},{66,2},{3,67},{67,3},{4,68},{68... | collective-permute-start | bytes 614408 | tf_op jit(solution)/shard_map/ppermute | solution.py:267
  3.3 1.3 %collective-permute-start.1 = (f32[80,128]{1,0:T(8,128)S(1)}, f32[80,128]{1,0:T(8,128)S(1)}, u32[]{:S(2)}, u32[]{:S(2)}) collective-permute-start(f32[80,128]{1,0:T(8,128)S(1)} %get-tuple-element.11), channel_id=1, source_target_pairs={{0,127},{1,64},{2,65},{3,66},{4,67},{5,68},{6,69},{7,70},{8,71},{9... | collective-permute-start | bytes 122888 | tf_op jit(solution)/shard_map/ppermute | solution.py:266
  4.6 7.2 %collective-permute-start.2 = (f32[80,128]{1,0:T(8,128)S(1)}, f32[80,128]{1,0:T(8,128)S(1)}, u32[]{:S(2)}, u32[]{:S(2)}) collective-permute-start(f32[80,128]{1,0:T(8,128)S(1)} %get-tuple-element.12), channel_id=1, source_target_pairs={{0,1},{1,2},{2,3},{3,4},{4,5},{5,6},{6,7},{7,8},{8,9},{9,10},{10,1... | collective-permute-start | bytes 122888 | tf_op jit(solution)/shard_map/ppermute | solution.py:265
  11.8 0.0 collective-permute-done.1.refs_2_
  11.8 1.1 %collective-permute-done.2.refs_3_ = f32[80,128]{1,0:T(8,128)S(1)} collective-permute-done((f32[80,128]{1,0:T(8,128)S(1)}, f32[80,128]{1,0:T(8,128)S(1)}, u32[]{:S(2)}, u32[]{:S(2)}) %collective-permute-start.2) | collective-permute-done | bytes 40992 | tf_op jit(solution)/shard_map/ppermute | solution.py:265
  12.9 0.0 collective-permute-done.refs_1_
  12.9 5.2 %shard_map.69 = (f32[16,64,128]{2,1,0:T(8,128)S(1)}, f32[16,64,128]{2,1,0:T(8,128)S(1)}, f32[128,2,128]{2,1,0:T(2,128)S(1)}) custom-call(s32[1]{0:T(128)} %bitcast.core_ref, f32[5,64,256]{2,1,0:T(8,128)S(1)} %get-tuple-element.9.refs_0_.held_ref, f32[400,128]{1,0:T(8,128)S(1)} %collective-permute-done.refs_1_, f32[80,128]{1,0:T(8,128)S(1)} %collective-permute-done.1.refs_2_, ...), custom_call_target="tpu_custom_call" | custom-call | tf_op jit(solution)/shard_map/pallas_call | solution.py:236
  18.1 8.8 %collective-permute-start.3 = (f32[16,64,128]{2,1,0:T(8,128)S(1)}, f32[16,64,128]{2,1,0:T(8,128)S(1)}, u32[]{:S(2)}, u32[]{:S(2)}) collective-permute-start(f32[16,64,128]{2,1,0:T(8,128)S(1)} %get-tuple-element.15), channel_id=1, source_target_pairs={{0,64},{64,0},{1,65},{65,1},{2,66},{66,2},{3,67},{67,3},{4,68},{68... | collective-permute-start | bytes 1572872 | tf_op jit(solution)/shard_map/ppermute | solution.py:279
  26.9 12.9 %all_to_all.5.sums_ref = f32[128,2,128]{2,1,0:T(2,128)S(1)} all-to-all(f32[128,2,128]{2,1,0:T(2,128)S(1)} %get-tuple-element.13), channel_id=1, replica_groups=mesh['gx'=2,'gy_0'=4,'gy_1'=4,'gy_2'=4] {'gx','gy_0','gy_1','gy_2'}, dimensions={0} | all-to-all | bytes 262144 | tf_op jit(solution)/shard_map/all_to_all | solution.py:280
  39.9 0.0 collective-permute-done.3.got_ref
  39.9 1.4 %shard_map.70 = (f32[64,256]{1,0:T(8,128)}, f32[64,256]{1,0:T(8,128)}) custom-call(s32[1]{0:T(128)} %bitcast.core_ref, f32[128,2,128]{2,1,0:T(2,128)S(1)} %all_to_all.5.sums_ref, f32[16,64,128]{2,1,0:T(8,128)S(1)} %get-tuple-element.14.own_ref, f32[16,64,128]{2,1,0:T(8,128)S(1)} %collective-permute-done.3.got_ref, ...), custom_call_target="tpu_custom_call" | custom-call | tf_op jit(solution)/shard_map/pallas_call | solution.py:236
Async XLA Ops:
  1.8 11.1 %collective-permute-start = (f32[400,128]{1,0:T(8,128)S(1)}, f32[400,128]{1,0:T(8,128)S(1)}, u32[]{:S(2)}, u32[]{:S(2)}) collective-permute-start(f32[400,128]{1,0:T(8,128)S(1)} %get-tuple-element.10), channel_id=1, source_target_pairs={{0,64},{64,0},{1,65},{65,1},{2,66},{66,2},{3,67},{67,3},{4,68},{68... | collective-permute-start | bytes 614408 | tf_op jit(solution)/shard_map/ppermute | solution.py:267
  3.3 8.5 %collective-permute-start.1 = (f32[80,128]{1,0:T(8,128)S(1)}, f32[80,128]{1,0:T(8,128)S(1)}, u32[]{:S(2)}, u32[]{:S(2)}) collective-permute-start(f32[80,128]{1,0:T(8,128)S(1)} %get-tuple-element.11), channel_id=1, source_target_pairs={{0,127},{1,64},{2,65},{3,66},{4,67},{5,68},{6,69},{7,70},{8,71},{9... | collective-permute-start | bytes 122888 | tf_op jit(solution)/shard_map/ppermute | solution.py:266
  4.6 8.3 %collective-permute-start.2 = (f32[80,128]{1,0:T(8,128)S(1)}, f32[80,128]{1,0:T(8,128)S(1)}, u32[]{:S(2)}, u32[]{:S(2)}) collective-permute-start(f32[80,128]{1,0:T(8,128)S(1)} %get-tuple-element.12), channel_id=1, source_target_pairs={{0,1},{1,2},{2,3},{3,4},{4,5},{5,6},{6,7},{7,8},{8,9},{9,10},{10,1... | collective-permute-start | bytes 122888 | tf_op jit(solution)/shard_map/ppermute | solution.py:265
  18.1 21.7 %collective-permute-start.3 = (f32[16,64,128]{2,1,0:T(8,128)S(1)}, f32[16,64,128]{2,1,0:T(8,128)S(1)}, u32[]{:S(2)}, u32[]{:S(2)}) collective-permute-start(f32[16,64,128]{2,1,0:T(8,128)S(1)} %get-tuple-element.15), channel_id=1, source_target_pairs={{0,64},{64,0},{1,65},{65,1},{2,66},{66,2},{3,67},{67,3},{4,68},{68... | collective-permute-start | bytes 1572872 | tf_op jit(solution)/shard_map/ppermute | solution.py:279

commit v4 on v3

--- a/solution.py
+++ b/solution.py
@@ -47,7 +47,8 @@
     return tiles + [jnp.concatenate(parts, axis=0)]
 
 
-def pack_body(core_ref, *refs):
+def pack_body(*refs):
+    mine_at = lax.axis_index("gx")
     fields, (same_ref, cross_ref, partner_ref, held_ref) = refs[:FIELDS], refs[FIELDS:]
     for a in range(FIELDS):
         held_ref[a] = fields[a][...]
@@ -58,7 +59,7 @@
 
     for core in (0, 1):
 
-        @pl.when(core_ref[0] == core)
+        @pl.when(mine_at == core)
         def _():
             left = [f[:, :LANES] for f in fields]
             right = [f[:, LANES:] for f in fields]
@@ -71,14 +72,15 @@
             put(same_ref, 0, right_edge if core == 0 else left_edge)
 
 
-def basis_body(core_ref, *refs):
+def basis_body(*refs):
+    mine_at = lax.axis_index("gx")
     held_ref, partner_ref, cross_ref, same_ref, own_ref, give_ref, gram_ref = refs[:7]
     data, coef, basis, image, pairs = refs[7:]
     lane = lax.broadcasted_iota(jnp.int32, (1, LANES), 1)
 
     for core in (0, 1):
 
-        @pl.when(core_ref[0] == core)
+        @pl.when(mine_at == core)
         def _():
             mine, beside = (slice(0, LANES), slice(LANES, COLS))
             if core:
@@ -158,7 +160,7 @@
                 return tuple(sums[4 * i + k] + first[i] * second[k] for i in range(4) for k in range(4))
 
             sums = lax.fori_loop(
-                0, FULL // 8, accumulate, tuple(jnp.zeros((8, LANES), jnp.float32) for _ in range(16)), unroll=2
+                0, FULL // 8, accumulate, tuple(jnp.zeros((8, LANES), jnp.float32) for _ in range(16)), unroll=8
             )
             for i in range(4):
                 for k in range(4):
@@ -179,7 +181,7 @@
     gram_ref[...] = jnp.broadcast_to(both[None], gram_ref.shape)
 
 
-def finish_body(core_ref, sums_ref, own_ref, got_ref, held_ref, solution_ref, residual_ref):
+def finish_body(sums_ref, own_ref, got_ref, held_ref, solution_ref, residual_ref):
     total = jnp.sum(sums_ref[...], axis=0)
     total = jnp.concatenate([total[0:1], total[1:2]], axis=1)
     lane = lax.broadcasted_iota(jnp.int32, (16, COLS), 1)
@@ -208,7 +210,7 @@
             value = value - SQUARE * z[k + 1]
         left.append(value)
     step = [SCALE * z[k] for k in range(RESTART)]
-    first = core_ref[0] == 0
+    first = lax.axis_index("gx") == 0
     for r in range(0, ROWS, 8):
         rows = slice(r, r + 8)
         sums = []
@@ -230,16 +232,16 @@
 def call(body, out_shape, scratch=(), staged=True):
     vmem = pl.BlockSpec(memory_space=pltpu.VMEM)
 
-    def run(core, *args):
+    def run(*args):
         if staged:
             args = [pltpu.with_memory_space_constraint(a, pltpu.VMEM) for a in args]
         return pl.pallas_call(
             body,
             out_shape=out_shape,
-            in_specs=[pl.BlockSpec(memory_space=pltpu.SMEM)] + [vmem] * len(args),
+            in_specs=[vmem] * len(args),
             out_specs=tuple(vmem for _ in out_shape),
             scratch_shapes=scratch,
-        )(core, *args)
+        )(*args)
 
     return run
 
@@ -250,7 +252,6 @@
 
 def per_device(right_side, initial, reaction, velocity_x, velocity_y):
     fields = (right_side, initial, reaction, velocity_x, velocity_y)
-    core = lax.axis_index("gx").astype(jnp.int32).reshape(1)
     count = lax.axis_size(GY)
     swap = [(0, 1), (1, 0)]
     ahead = lambda g: (g + 1) % count
@@ -261,7 +262,7 @@
     edge = on_chip(ROWS + 16, LANES)
     to_same, to_cross, to_partner, held = call(
         pack_body, (edge, edge, on_chip(FIELDS * ROWS + ROWS + 16, LANES), on_chip(FIELDS, ROWS, COLS)), staged=False
-    )(core, *fields)
+    )(*fields)
     from_same = lax.ppermute(to_same, ALL, same)
     from_cross = lax.ppermute(to_cross, ALL, cross)
     from_partner = lax.ppermute(to_partner, "gx", swap)
@@ -275,11 +276,11 @@
             on_chip(16, FULL, LANES),
             on_chip(COLS, LANES),
         ],
-    )(core, held, from_partner, from_cross, from_same)
+    )(held, from_partner, from_cross, from_same)
     got = lax.ppermute(give, "gx", swap)
     sums = lax.all_to_all(gram, ALL, 0, 0, tiled=True)
     result = jax.ShapeDtypeStruct((ROWS, COLS), jnp.float32)
-    return call(finish_body, (result, result))(core, sums, own, got, held)
+    return call(finish_body, (result, result))(sums, own, got, held)
 
 
 def solution(mesh):

time: 41.4 us -> 41 us (level)
  no operation moved by 1% of the time
where the time goes in v4:
time: 41 us; the launch traced here: 40.9 us
  starting transfers between devices  18.8 us (46%)
  blocking collectives  12.9 us (31%)
  Pallas kernels  7.39 us (18%)
  waiting for transfers between devices  1.11 us (3%)
  between operations  0.65 us (2%)
    all_to_all x1, blocking collectives, per_device(): sums = lax.all_to_all(gram, ALL, 0, 0, tiled=True)  12.9 us
    ppermute x1, starting transfers between devices, per_device(): got = lax.ppermute(give, 'gx', swap)  8.8 us
    pallas_call x3, Pallas kernels, run(): pl.pallas_call(body, out_shape=out_shape, in_specs=[vmem] * len(args), ou...  7.39 us
    ppermute x1, starting transfers between devices, per_device(): from_same = lax.ppermute(to_same, ALL, same)  7.22 us
    ppermute x1, starting transfers between devices, per_device(): from_partner = lax.ppermute(to_partner, 'gx', swap)  1.47 us
    ppermute x1, starting transfers between devices, per_device(): from_cross = lax.ppermute(to_cross, ALL, cross)  1.3 us
    ppermute x1, waiting for transfers between devices, per_device(): from_same = lax.ppermute(to_same, ALL, same)  1.1 us
  transfers between devices with their start and end apart: 4, of which 1 were waited for; matrix products, arithmetic and copies ran while one was open for 0% of the time, Pallas kernels for 0%

profile of v4, /device:TPU:1, one launch (start us, length us, event | category | flops | bytes accessed | tf_op | source)
XLA Modules:
  0.0 40.9 jit_solution(14769658561574941709)
XLA Ops:
  0.6 1.1 %shard_map.68 = (f32[80,128]{1,0:T(8,128)S(1)}, f32[80,128]{1,0:T(8,128)S(1)}, f32[400,128]{1,0:T(8,128)S(1)}, f32[5,64,256]{2,1,0:T(8,128)S(1)}) custom-call(f32[64,256]{1,0:T(8,128)} %refs_0_.1, f32[64,256]{1,0:T(8,128)} %refs_1_.1, f32[64,256]{1,0:T(8,128)} %refs_2_.1, f32[64,256]{1,0:T(8,128)} %refs_3_.1, f32[64,256]{1,0:T(8,128)} %refs_4_.1), custom_call_target="tpu_custom_call" | custom-call | tf_op jit(solution)/shard_map/pallas_call | solution.py:238
  1.8 1.5 %collective-permute-start = (f32[400,128]{1,0:T(8,128)S(1)}, f32[400,128]{1,0:T(8,128)S(1)}, u32[]{:S(2)}, u32[]{:S(2)}) collective-permute-start(f32[400,128]{1,0:T(8,128)S(1)} %get-tuple-element.10), channel_id=1, source_target_pairs={{0,64},{64,0},{1,65},{65,1},{2,66},{66,2},{3,67},{67,3},{4,68},{68... | collective-permute-start | bytes 614408 | tf_op jit(solution)/shard_map/ppermute | solution.py:268
  3.3 1.3 %collective-permute-start.1 = (f32[80,128]{1,0:T(8,128)S(1)}, f32[80,128]{1,0:T(8,128)S(1)}, u32[]{:S(2)}, u32[]{:S(2)}) collective-permute-start(f32[80,128]{1,0:T(8,128)S(1)} %get-tuple-element.11), channel_id=1, source_target_pairs={{0,127},{1,64},{2,65},{3,66},{4,67},{5,68},{6,69},{7,70},{8,71},{9... | collective-permute-start | bytes 122888 | tf_op jit(solution)/shard_map/ppermute | solution.py:267
  4.6 7.2 %collective-permute-start.2 = (f32[80,128]{1,0:T(8,128)S(1)}, f32[80,128]{1,0:T(8,128)S(1)}, u32[]{:S(2)}, u32[]{:S(2)}) collective-permute-start(f32[80,128]{1,0:T(8,128)S(1)} %get-tuple-element.12), channel_id=1, source_target_pairs={{0,1},{1,2},{2,3},{3,4},{4,5},{5,6},{6,7},{7,8},{8,9},{9,10},{10,1... | collective-permute-start | bytes 122888 | tf_op jit(solution)/shard_map/ppermute | solution.py:266
  11.8 0.0 collective-permute-done.1.refs_2_
  11.8 1.1 %collective-permute-done.2.refs_3_ = f32[80,128]{1,0:T(8,128)S(1)} collective-permute-done((f32[80,128]{1,0:T(8,128)S(1)}, f32[80,128]{1,0:T(8,128)S(1)}, u32[]{:S(2)}, u32[]{:S(2)}) %collective-permute-start.2) | collective-permute-done | bytes 40992 | tf_op jit(solution)/shard_map/ppermute | solution.py:266
  12.9 0.0 collective-permute-done.refs_1_
  12.9 4.9 %shard_map.69 = (f32[16,64,128]{2,1,0:T(8,128)S(1)}, f32[16,64,128]{2,1,0:T(8,128)S(1)}, f32[128,2,128]{2,1,0:T(2,128)S(1)}) custom-call(f32[5,64,256]{2,1,0:T(8,128)S(1)} %get-tuple-element.9.refs_0_.held_ref, f32[400,128]{1,0:T(8,128)S(1)} %collective-permute-done.refs_1_, f32[80,128]{1,0:T(8,128)S(1)} %collective-permute-done.1.refs_2_, ...), custom_call_target="tpu_custom_call" | custom-call | tf_op jit(solution)/shard_map/pallas_call | solution.py:238
  17.8 8.8 %collective-permute-start.3 = (f32[16,64,128]{2,1,0:T(8,128)S(1)}, f32[16,64,128]{2,1,0:T(8,128)S(1)}, u32[]{:S(2)}, u32[]{:S(2)}) collective-permute-start(f32[16,64,128]{2,1,0:T(8,128)S(1)} %get-tuple-element.15), channel_id=1, source_target_pairs={{0,64},{64,0},{1,65},{65,1},{2,66},{66,2},{3,67},{67,3},{4,68},{68... | collective-permute-start | bytes 1572872 | tf_op jit(solution)/shard_map/ppermute | solution.py:280
  26.6 12.9 %all_to_all.5.sums_ref = f32[128,2,128]{2,1,0:T(2,128)S(1)} all-to-all(f32[128,2,128]{2,1,0:T(2,128)S(1)} %get-tuple-element.13), channel_id=1, replica_groups=mesh['gx'=2,'gy_0'=4,'gy_1'=4,'gy_2'=4] {'gx','gy_0','gy_1','gy_2'}, dimensions={0} | all-to-all | bytes 262144 | tf_op jit(solution)/shard_map/all_to_all | solution.py:281
  39.5 0.0 collective-permute-done.3.got_ref
  39.5 1.4 %shard_map.70 = (f32[64,256]{1,0:T(8,128)}, f32[64,256]{1,0:T(8,128)}) custom-call(f32[128,2,128]{2,1,0:T(2,128)S(1)} %all_to_all.5.sums_ref, f32[16,64,128]{2,1,0:T(8,128)S(1)} %get-tuple-element.14.own_ref, f32[16,64,128]{2,1,0:T(8,128)S(1)} %collective-permute-done.3.got_ref, f32[5,64,256]{2,1,0:T(8,128)S(1)} %get-tuple-element.9.refs_0_.held_ref), custom_call_target="tpu_custom_call" | custom-call | tf_op jit(solution)/shard_map/pallas_call | solution.py:238
Async XLA Ops:
  1.8 11.1 %collective-permute-start = (f32[400,128]{1,0:T(8,128)S(1)}, f32[400,128]{1,0:T(8,128)S(1)}, u32[]{:S(2)}, u32[]{:S(2)}) collective-permute-start(f32[400,128]{1,0:T(8,128)S(1)} %get-tuple-element.10), channel_id=1, source_target_pairs={{0,64},{64,0},{1,65},{65,1},{2,66},{66,2},{3,67},{67,3},{4,68},{68... | collective-permute-start | bytes 614408 | tf_op jit(solution)/shard_map/ppermute | solution.py:268
  3.3 8.5 %collective-permute-start.1 = (f32[80,128]{1,0:T(8,128)S(1)}, f32[80,128]{1,0:T(8,128)S(1)}, u32[]{:S(2)}, u32[]{:S(2)}) collective-permute-start(f32[80,128]{1,0:T(8,128)S(1)} %get-tuple-element.11), channel_id=1, source_target_pairs={{0,127},{1,64},{2,65},{3,66},{4,67},{5,68},{6,69},{7,70},{8,71},{9... | collective-permute-start | bytes 122888 | tf_op jit(solution)/shard_map/ppermute | solution.py:267
  4.6 8.3 %collective-permute-start.2 = (f32[80,128]{1,0:T(8,128)S(1)}, f32[80,128]{1,0:T(8,128)S(1)}, u32[]{:S(2)}, u32[]{:S(2)}) collective-permute-start(f32[80,128]{1,0:T(8,128)S(1)} %get-tuple-element.12), channel_id=1, source_target_pairs={{0,1},{1,2},{2,3},{3,4},{4,5},{5,6},{6,7},{7,8},{8,9},{9,10},{10,1... | collective-permute-start | bytes 122888 | tf_op jit(solution)/shard_map/ppermute | solution.py:266
  17.8 21.7 %collective-permute-start.3 = (f32[16,64,128]{2,1,0:T(8,128)S(1)}, f32[16,64,128]{2,1,0:T(8,128)S(1)}, u32[]{:S(2)}, u32[]{:S(2)}) collective-permute-start(f32[16,64,128]{2,1,0:T(8,128)S(1)} %get-tuple-element.15), channel_id=1, source_target_pairs={{0,64},{64,0},{1,65},{65,1},{2,66},{66,2},{3,67},{67,3},{4,68},{68... | collective-permute-start | bytes 1572872 | tf_op jit(solution)/shard_map/ppermute | solution.py:280

commit v5 on v4

--- a/solution.py
+++ b/solution.py
@@ -91,64 +91,78 @@
             cross = unpacked_edges(cross_ref, 0, far)
             inner = unpacked_edges(partner_ref, FIELDS * ROWS, near)
             for a in range(FIELDS):
-                data[a, 8 : 8 + ROWS, :LANES] = held_ref[a, :, mine]
-                data[a, 8 + ROWS : 8 + FULL, :LANES] = partner_ref[ROWS * a : ROWS * (a + 1), :]
+                data[a, 0, 8 : 8 + ROWS, :] = held_ref[a, :, mine]
+                data[a, 0, 8 + ROWS : 8 + FULL, :] = partner_ref[ROWS * a : ROWS * (a + 1), :]
                 for row, here, there in ((8, held_ref[a, :, beside], same[a]), (8 + ROWS, inner[a], cross[a])):
                     low, high = (here, there) if core == 0 else (there, here)
                     tile = jnp.where(lane < HALO, low, jnp.where(lane >= LANES - HALO, high, 0.0))
-                    data[a, row : row + ROWS, LANES:] = tile
+                    data[a, 1, row : row + ROWS, :] = tile
+
+    def turned(tiles, shift):
+        one, two = (pltpu.roll(tile, shift % LANES, 1) for tile in tiles)
+        over = lane < shift if shift > 0 else lane >= LANES + shift
+        return jnp.where(over, two, one), jnp.where(over, one, two)
+
+    def wrap(ref, index):
+        for t in (0, 1):
+            ref[index, t, 0:8, :] = ref[index, t, FULL : FULL + 8, :]
+            ref[index, t, 8 + FULL : 16 + FULL, :] = ref[index, t, 8:16, :]
+
+    def shifted(ref, index, r, o):
+        return [ref[index, t, 8 + r + o : 24 + r + o, :] for t in (0, 1)]
 
     for a in range(FIELDS):
-        data[a, 0:8, :] = data[a, FULL : FULL + 8, :]
-        data[a, 8 + FULL : 16 + FULL, :] = data[a, 8:16, :]
+        wrap(data, a)
 
     for r in range(0, FULL, 16):
         rows = slice(r, r + 16)
-        at = lambda a, o: data[a, 8 + r + o : 24 + r + o, :]
-        coef[0, rows, :] = SCALE * (at(2, 0) + (5.0 - CENTRE))
-        vx, vy = at(3, 0), at(4, 0)
+        middle, vx, vy = (shifted(data, a, r, 0) for a in (2, 3, 4))
+        for t in (0, 1):
+            coef[0, t, rows, :] = SCALE * (middle[t] + (5.0 - CENTRE))
         for o in (1, 2):
             base = SCALE * (-4.0 / 3.0 if o == 1 else 1.0 / 12.0)
             turn = SCALE * (1.0 / 3.0 if o == 1 else -1.0 / 24.0)
-            coef[4 * o - 3, rows, :] = base + turn * (vx + at(3, o))
-            coef[4 * o - 2, rows, :] = base - turn * (vx + at(3, -o))
-            coef[4 * o - 1, rows, :] = base + turn * (vy + pltpu.roll(vy, COLS - o, 1))
-            coef[4 * o, rows, :] = base - turn * (vy + pltpu.roll(vy, o, 1))
-
-    def stencil(load, r):
+            below, above = shifted(data, 3, r, o), shifted(data, 3, r, -o)
+            ahead, behind = turned(vy, -o), turned(vy, o)
+            for t in (0, 1):
+                coef[4 * o - 3, t, rows, :] = base + turn * (vx[t] + below[t])
+                coef[4 * o - 2, t, rows, :] = base - turn * (vx[t] + above[t])
+                coef[4 * o - 1, t, rows, :] = base + turn * (vy[t] + ahead[t])
+                coef[4 * o, t, rows, :] = base - turn * (vy[t] + behind[t])
+
+    def stencil(ref, index, r):
         rows = slice(r, r + 16)
-        field = load(0)
-        total = coef[0, rows, :] * field
+        field = shifted(ref, index, r, 0)
+        total = [coef[0, t, rows, :] * field[t] for t in (0, 1)]
         for o in (1, 2):
-            total += coef[4 * o - 3, rows, :] * load(o)
-            total += coef[4 * o - 2, rows, :] * load(-o)
-            total += coef[4 * o - 1, rows, :] * pltpu.roll(field, COLS - o, 1)
-            total += coef[4 * o, rows, :] * pltpu.roll(field, o, 1)
+            moved = (shifted(ref, index, r, o), shifted(ref, index, r, -o), turned(field, -o), turned(field, o))
+            for k, tiles in enumerate(moved):
+                total = [total[t] + coef[4 * o - 3 + k, t, rows, :] * tiles[t] for t in (0, 1)]
         return field, total
 
-    def wrap(index):
-        basis[index, 0:8, :] = basis[index, FULL : FULL + 8, :]
-        basis[index, 8 + FULL : 16 + FULL, :] = basis[index, 8:16, :]
-
-    basis[0, 8 : 8 + FULL, :] = jnp.zeros((FULL, COLS), jnp.float32)
+    for t in (0, 1):
+        basis[0, t, 8 : 8 + FULL, :] = jnp.zeros((FULL, LANES), jnp.float32)
     for r in range(0, FULL, 16):
-        field, total = stencil(lambda o: data[1, 8 + r + o : 24 + r + o, :], r)
-        start = data[0, 8 + r : 24 + r, :] - ((1.0 / SCALE) * total + CENTRE * field)
-        basis[1, 8 + r : 24 + r, :] = start
-        image[RESTART, r : r + 16, :] = start[:, :LANES]
-    wrap(1)
+        field, total = stencil(data, 1, r)
+        for t in (0, 1):
+            start = data[0, t, 8 + r : 24 + r, :] - ((1.0 / SCALE) * total[t] + CENTRE * field[t])
+            basis[1, t, 8 + r : 24 + r, :] = start
+            if t == 0:
+                image[RESTART, r : r + 16, :] = start
+    wrap(basis, 1)
 
     def step(j, carried):
         for r in range(0, FULL, 16):
-            field, total = stencil(lambda o: basis[j + 1, 8 + r + o : 24 + r + o, :], r)
-            image[j, r : r + 16, :] = total[:, :LANES] + ALPHA * field[:, :LANES]
-            basis[j + 2, 8 + r : 24 + r, :] = total - SQUARE * basis[j, 8 + r : 24 + r, :]
-        wrap(j + 2)
+            field, total = stencil(basis, j + 1, r)
+            image[j, r : r + 16, :] = total[0] + ALPHA * field[0]
+            for t in (0, 1):
+                basis[j + 2, t, 8 + r : 24 + r, :] = total[t] - SQUARE * basis[j, t, 8 + r : 24 + r, :]
+        wrap(basis, j + 2)
         return carried
 
     lax.fori_loop(0, RESTART, step, 0)
-    own_ref[...] = basis[1:, 8 : 8 + ROWS, :LANES]
-    give_ref[...] = basis[1:, 8 + ROWS : 8 + FULL, :LANES]
+    own_ref[...] = basis[1:, 0, 8 : 8 + ROWS, :]
+    give_ref[...] = basis[1:, 0, 8 + ROWS : 8 + FULL, :]
 
     for low in range(0, 16, 4):
         for high in range(low, 16, 4):
@@ -270,9 +284,9 @@
         basis_body,
         (on_chip(16, ROWS, LANES), on_chip(16, ROWS, LANES), on_chip(2 * count, 2, LANES)),
         scratch=[
-            on_chip(FIELDS, FULL + 16, COLS),
-            on_chip(9, FULL, COLS),
-            on_chip(RESTART + 2, FULL + 16, COLS),
+            on_chip(FIELDS, 2, FULL + 16, LANES),
+            on_chip(9, 2, FULL, LANES),
+            on_chip(RESTART + 2, 2, FULL + 16, LANES),
             on_chip(16, FULL, LANES),
             on_chip(COLS, LANES),
         ],

time: 41 us -> 41 us (level)
  no operation moved by 1% of the time
where the time goes in v5:
time: 41 us; the launch traced here: 40.8 us
  starting transfers between devices  18.8 us (46%)
  blocking collectives  12.9 us (31%)
  Pallas kernels  7.32 us (18%)
  waiting for transfers between devices  1.11 us (3%)
  between operations  0.65 us (2%)
    all_to_all x1, blocking collectives, per_device(): sums = lax.all_to_all(gram, ALL, 0, 0, tiled=True)  12.9 us
    ppermute x1, starting transfers between devices, per_device(): got = lax.ppermute(give, 'gx', swap)  8.8 us
    pallas_call x3, Pallas kernels, run(): pl.pallas_call(body, out_shape=out_shape, in_specs=[vmem] * len(args), ou...  7.32 us
    ppermute x1, starting transfers between devices, per_device(): from_same = lax.ppermute(to_same, ALL, same)  7.22 us
    ppermute x1, starting transfers between devices, per_device(): from_partner = lax.ppermute(to_partner, 'gx', swap)  1.47 us
    ppermute x1, starting transfers between devices, per_device(): from_cross = lax.ppermute(to_cross, ALL, cross)  1.3 us
    ppermute x1, waiting for transfers between devices, per_device(): from_same = lax.ppermute(to_same, ALL, same)  1.1 us
  transfers between devices with their start and end apart: 4, of which 1 were waited for; matrix products, arithmetic and copies ran while one was open for 0% of the time, Pallas kernels for 0%

profile of v5, /device:TPU:1, one launch (start us, length us, event | category | flops | bytes accessed | tf_op | source)
XLA Modules:
  0.0 40.8 jit_solution(9772983968359726933)
XLA Ops:
  0.6 1.1 %shard_map.68 = (f32[80,128]{1,0:T(8,128)S(1)}, f32[80,128]{1,0:T(8,128)S(1)}, f32[400,128]{1,0:T(8,128)S(1)}, f32[5,64,256]{2,1,0:T(8,128)S(1)}) custom-call(f32[64,256]{1,0:T(8,128)} %refs_0_.1, f32[64,256]{1,0:T(8,128)} %refs_1_.1, f32[64,256]{1,0:T(8,128)} %refs_2_.1, f32[64,256]{1,0:T(8,128)} %refs_3_.1, f32[64,256]{1,0:T(8,128)} %refs_4_.1), custom_call_target="tpu_custom_call" | custom-call | tf_op jit(solution)/shard_map/pallas_call | solution.py:252
  1.8 1.5 %collective-permute-start = (f32[400,128]{1,0:T(8,128)S(1)}, f32[400,128]{1,0:T(8,128)S(1)}, u32[]{:S(2)}, u32[]{:S(2)}) collective-permute-start(f32[400,128]{1,0:T(8,128)S(1)} %get-tuple-element.10), channel_id=1, source_target_pairs={{0,64},{64,0},{1,65},{65,1},{2,66},{66,2},{3,67},{67,3},{4,68},{68... | collective-permute-start | bytes 614408 | tf_op jit(solution)/shard_map/ppermute | solution.py:282
  3.3 1.3 %collective-permute-start.1 = (f32[80,128]{1,0:T(8,128)S(1)}, f32[80,128]{1,0:T(8,128)S(1)}, u32[]{:S(2)}, u32[]{:S(2)}) collective-permute-start(f32[80,128]{1,0:T(8,128)S(1)} %get-tuple-element.11), channel_id=1, source_target_pairs={{0,127},{1,64},{2,65},{3,66},{4,67},{5,68},{6,69},{7,70},{8,71},{9... | collective-permute-start | bytes 122888 | tf_op jit(solution)/shard_map/ppermute | solution.py:281
  4.6 7.2 %collective-permute-start.2 = (f32[80,128]{1,0:T(8,128)S(1)}, f32[80,128]{1,0:T(8,128)S(1)}, u32[]{:S(2)}, u32[]{:S(2)}) collective-permute-start(f32[80,128]{1,0:T(8,128)S(1)} %get-tuple-element.12), channel_id=1, source_target_pairs={{0,1},{1,2},{2,3},{3,4},{4,5},{5,6},{6,7},{7,8},{8,9},{9,10},{10,1... | collective-permute-start | bytes 122888 | tf_op jit(solution)/shard_map/ppermute | solution.py:280
  11.8 0.0 collective-permute-done.1.refs_2_
  11.8 1.1 %collective-permute-done.2.refs_3_ = f32[80,128]{1,0:T(8,128)S(1)} collective-permute-done((f32[80,128]{1,0:T(8,128)S(1)}, f32[80,128]{1,0:T(8,128)S(1)}, u32[]{:S(2)}, u32[]{:S(2)}) %collective-permute-start.2) | collective-permute-done | bytes 40992 | tf_op jit(solution)/shard_map/ppermute | solution.py:280
  12.9 0.0 collective-permute-done.refs_1_
  12.9 4.8 %shard_map.69 = (f32[16,64,128]{2,1,0:T(8,128)S(1)}, f32[16,64,128]{2,1,0:T(8,128)S(1)}, f32[128,2,128]{2,1,0:T(2,128)S(1)}) custom-call(f32[5,64,256]{2,1,0:T(8,128)S(1)} %get-tuple-element.9.refs_0_.held_ref, f32[400,128]{1,0:T(8,128)S(1)} %collective-permute-done.refs_1_, f32[80,128]{1,0:T(8,128)S(1)} %collective-permute-done.1.refs_2_, ...), custom_call_target="tpu_custom_call" | custom-call | tf_op jit(solution)/shard_map/pallas_call | solution.py:252
  17.7 8.8 %collective-permute-start.3 = (f32[16,64,128]{2,1,0:T(8,128)S(1)}, f32[16,64,128]{2,1,0:T(8,128)S(1)}, u32[]{:S(2)}, u32[]{:S(2)}) collective-permute-start(f32[16,64,128]{2,1,0:T(8,128)S(1)} %get-tuple-element.15), channel_id=1, source_target_pairs={{0,64},{64,0},{1,65},{65,1},{2,66},{66,2},{3,67},{67,3},{4,68},{68... | collective-permute-start | bytes 1572872 | tf_op jit(solution)/shard_map/ppermute | solution.py:294
  26.5 12.9 %all_to_all.5.sums_ref = f32[128,2,128]{2,1,0:T(2,128)S(1)} all-to-all(f32[128,2,128]{2,1,0:T(2,128)S(1)} %get-tuple-element.13), channel_id=1, replica_groups=mesh['gx'=2,'gy_0'=4,'gy_1'=4,'gy_2'=4] {'gx','gy_0','gy_1','gy_2'}, dimensions={0} | all-to-all | bytes 262144 | tf_op jit(solution)/shard_map/all_to_all | solution.py:295
  39.4 0.0 collective-permute-done.3.got_ref
  39.4 1.4 %shard_map.70 = (f32[64,256]{1,0:T(8,128)}, f32[64,256]{1,0:T(8,128)}) custom-call(f32[128,2,128]{2,1,0:T(2,128)S(1)} %all_to_all.5.sums_ref, f32[16,64,128]{2,1,0:T(8,128)S(1)} %get-tuple-element.14.own_ref, f32[16,64,128]{2,1,0:T(8,128)S(1)} %collective-permute-done.3.got_ref, f32[5,64,256]{2,1,0:T(8,128)S(1)} %get-tuple-element.9.refs_0_.held_ref), custom_call_target="tpu_custom_call" | custom-call | tf_op jit(solution)/shard_map/pallas_call | solution.py:252
Async XLA Ops:
  1.8 11.1 %collective-permute-start = (f32[400,128]{1,0:T(8,128)S(1)}, f32[400,128]{1,0:T(8,128)S(1)}, u32[]{:S(2)}, u32[]{:S(2)}) collective-permute-start(f32[400,128]{1,0:T(8,128)S(1)} %get-tuple-element.10), channel_id=1, source_target_pairs={{0,64},{64,0},{1,65},{65,1},{2,66},{66,2},{3,67},{67,3},{4,68},{68... | collective-permute-start | bytes 614408 | tf_op jit(solution)/shard_map/ppermute | solution.py:282
  3.3 8.5 %collective-permute-start.1 = (f32[80,128]{1,0:T(8,128)S(1)}, f32[80,128]{1,0:T(8,128)S(1)}, u32[]{:S(2)}, u32[]{:S(2)}) collective-permute-start(f32[80,128]{1,0:T(8,128)S(1)} %get-tuple-element.11), channel_id=1, source_target_pairs={{0,127},{1,64},{2,65},{3,66},{4,67},{5,68},{6,69},{7,70},{8,71},{9... | collective-permute-start | bytes 122888 | tf_op jit(solution)/shard_map/ppermute | solution.py:281
  4.6 8.3 %collective-permute-start.2 = (f32[80,128]{1,0:T(8,128)S(1)}, f32[80,128]{1,0:T(8,128)S(1)}, u32[]{:S(2)}, u32[]{:S(2)}) collective-permute-start(f32[80,128]{1,0:T(8,128)S(1)} %get-tuple-element.12), channel_id=1, source_target_pairs={{0,1},{1,2},{2,3},{3,4},{4,5},{5,6},{6,7},{7,8},{8,9},{9,10},{10,1... | collective-permute-start | bytes 122888 | tf_op jit(solution)/shard_map/ppermute | solution.py:280
  17.7 21.7 %collective-permute-start.3 = (f32[16,64,128]{2,1,0:T(8,128)S(1)}, f32[16,64,128]{2,1,0:T(8,128)S(1)}, u32[]{:S(2)}, u32[]{:S(2)}) collective-permute-start(f32[16,64,128]{2,1,0:T(8,128)S(1)} %get-tuple-element.15), channel_id=1, source_target_pairs={{0,64},{64,0},{1,65},{65,1},{2,66},{66,2},{3,67},{67,3},{4,68},{68... | collective-permute-start | bytes 1572872 | tf_op jit(solution)/shard_map/ppermute | solution.py:294

commit v6 on v5

--- a/solution.py
+++ b/solution.py
@@ -75,7 +75,7 @@
 def basis_body(*refs):
     mine_at = lax.axis_index("gx")
     held_ref, partner_ref, cross_ref, same_ref, own_ref, give_ref, gram_ref = refs[:7]
-    data, coef, basis, image, pairs = refs[7:]
+    data, coef, image, pairs, *turns = refs[7:]
     lane = lax.broadcasted_iota(jnp.int32, (1, LANES), 1)
 
     for core in (0, 1):
@@ -140,29 +140,40 @@
                 total = [total[t] + coef[4 * o - 3 + k, t, rows, :] * tiles[t] for t in (0, 1)]
         return field, total
 
+    def keep(k, r, tile):
+        if r < ROWS:
+            own_ref[k, r : r + 16, :] = tile
+        else:
+            give_ref[k, r - ROWS : r - ROWS + 16, :] = tile
+
     for t in (0, 1):
-        basis[0, t, 8 : 8 + FULL, :] = jnp.zeros((FULL, LANES), jnp.float32)
+        turns[0][0, t, 8 : 8 + FULL, :] = jnp.zeros((FULL, LANES), jnp.float32)
     for r in range(0, FULL, 16):
         field, total = stencil(data, 1, r)
         for t in (0, 1):
             start = data[0, t, 8 + r : 24 + r, :] - ((1.0 / SCALE) * total[t] + CENTRE * field[t])
-            basis[1, t, 8 + r : 24 + r, :] = start
+            turns[1][0, t, 8 + r : 24 + r, :] = start
             if t == 0:
                 image[RESTART, r : r + 16, :] = start
-    wrap(basis, 1)
-
-    def step(j, carried):
-        for r in range(0, FULL, 16):
-            field, total = stencil(basis, j + 1, r)
-            image[j, r : r + 16, :] = total[0] + ALPHA * field[0]
-            for t in (0, 1):
-                basis[j + 2, t, 8 + r : 24 + r, :] = total[t] - SQUARE * basis[j, t, 8 + r : 24 + r, :]
-        wrap(basis, j + 2)
+                keep(0, r, start)
+    wrap(turns[1], 0)
+
+    def steps(third, carried):
+        for u in range(3):
+            j = 3 * third + u
+            past, now, later = turns[u], turns[(u + 1) % 3], turns[(u + 2) % 3]
+            for r in range(0, FULL, 16):
+                field, total = stencil(now, 0, r)
+                image[j, r : r + 16, :] = total[0] + ALPHA * field[0]
+                for t in (0, 1):
+                    tile = total[t] - SQUARE * past[0, t, 8 + r : 24 + r, :]
+                    later[0, t, 8 + r : 24 + r, :] = tile
+                    if t == 0:
+                        keep(j + 1, r, tile)
+            wrap(later, 0)
         return carried
 
-    lax.fori_loop(0, RESTART, step, 0)
-    own_ref[...] = basis[1:, 0, 8 : 8 + ROWS, :]
-    give_ref[...] = basis[1:, 0, 8 + ROWS : 8 + FULL, :]
+    lax.fori_loop(0, RESTART // 3, steps, 0)
 
     for low in range(0, 16, 4):
         for high in range(low, 16, 4):
@@ -286,9 +297,9 @@
         scratch=[
             on_chip(FIELDS, 2, FULL + 16, LANES),
             on_chip(9, 2, FULL, LANES),
-            on_chip(RESTART + 2, 2, FULL + 16, LANES),
             on_chip(16, FULL, LANES),
             on_chip(COLS, LANES),
+            *(on_chip(1, 2, FULL + 16, LANES) for _ in range(3)),
         ],
     )(held, from_partner, from_cross, from_same)
     got = lax.ppermute(give, "gx", swap)

time: 41 us -> 40.2 us (0.980)
  Pallas kernels: 7.32 us -> 6.5 us
    pallas_call x3, Pallas kernels: 7.32 us -> 6.5 us  [run(): pl.pallas_call(body, out_shape=out_shape, in_specs=[vmem] * len(args), ou...]
where the time goes in v6:
time: 40.2 us; the launch traced here: 40 us
  starting transfers between devices  18.8 us (47%)
  blocking collectives  12.9 us (32%)
  Pallas kernels  6.5 us (16%)
  waiting for transfers between devices  1.11 us (3%)
  between operations  0.65 us (2%)
    all_to_all x1, blocking collectives, per_device(): sums = lax.all_to_all(gram, ALL, 0, 0, tiled=True)  12.9 us
    ppermute x1, starting transfers between devices, per_device(): got = lax.ppermute(give, 'gx', swap)  8.8 us
    ppermute x1, starting transfers between devices, per_device(): from_same = lax.ppermute(to_same, ALL, same)  7.22 us
    pallas_call x3, Pallas kernels, run(): pl.pallas_call(body, out_shape=out_shape, in_specs=[vmem] * len(args), ou...  6.5 us
    ppermute x1, starting transfers between devices, per_device(): from_partner = lax.ppermute(to_partner, 'gx', swap)  1.47 us
    ppermute x1, starting transfers between devices, per_device(): from_cross = lax.ppermute(to_cross, ALL, cross)  1.3 us
    ppermute x1, waiting for transfers between devices, per_device(): from_same = lax.ppermute(to_same, ALL, same)  1.1 us
  transfers between devices with their start and end apart: 4, of which 1 were waited for; matrix products, arithmetic and copies ran while one was open for 0% of the time, Pallas kernels for 0%

profile of v6, /device:TPU:1, one launch (start us, length us, event | category | flops | bytes accessed | tf_op | source)
XLA Modules:
  0.0 40.0 jit_solution(11515993145895771195)
XLA Ops:
  0.6 1.1 %shard_map.68 = (f32[80,128]{1,0:T(8,128)S(1)}, f32[80,128]{1,0:T(8,128)S(1)}, f32[400,128]{1,0:T(8,128)S(1)}, f32[5,64,256]{2,1,0:T(8,128)S(1)}) custom-call(f32[64,256]{1,0:T(8,128)} %refs_0_.1, f32[64,256]{1,0:T(8,128)} %refs_1_.1, f32[64,256]{1,0:T(8,128)} %refs_2_.1, f32[64,256]{1,0:T(8,128)} %refs_3_.1, f32[64,256]{1,0:T(8,128)} %refs_4_.1), custom_call_target="tpu_custom_call" | custom-call | tf_op jit(solution)/shard_map/pallas_call | solution.py:263
  1.8 1.5 %collective-permute-start = (f32[400,128]{1,0:T(8,128)S(1)}, f32[400,128]{1,0:T(8,128)S(1)}, u32[]{:S(2)}, u32[]{:S(2)}) collective-permute-start(f32[400,128]{1,0:T(8,128)S(1)} %get-tuple-element.10), channel_id=1, source_target_pairs={{0,64},{64,0},{1,65},{65,1},{2,66},{66,2},{3,67},{67,3},{4,68},{68... | collective-permute-start | bytes 614408 | tf_op jit(solution)/shard_map/ppermute | solution.py:293
  3.3 1.3 %collective-permute-start.1 = (f32[80,128]{1,0:T(8,128)S(1)}, f32[80,128]{1,0:T(8,128)S(1)}, u32[]{:S(2)}, u32[]{:S(2)}) collective-permute-start(f32[80,128]{1,0:T(8,128)S(1)} %get-tuple-element.11), channel_id=1, source_target_pairs={{0,127},{1,64},{2,65},{3,66},{4,67},{5,68},{6,69},{7,70},{8,71},{9... | collective-permute-start | bytes 122888 | tf_op jit(solution)/shard_map/ppermute | solution.py:292
  4.6 7.2 %collective-permute-start.2 = (f32[80,128]{1,0:T(8,128)S(1)}, f32[80,128]{1,0:T(8,128)S(1)}, u32[]{:S(2)}, u32[]{:S(2)}) collective-permute-start(f32[80,128]{1,0:T(8,128)S(1)} %get-tuple-element.12), channel_id=1, source_target_pairs={{0,1},{1,2},{2,3},{3,4},{4,5},{5,6},{6,7},{7,8},{8,9},{9,10},{10,1... | collective-permute-start | bytes 122888 | tf_op jit(solution)/shard_map/ppermute | solution.py:291
  11.8 0.0 collective-permute-done.1.refs_2_
  11.8 1.1 %collective-permute-done.2.refs_3_ = f32[80,128]{1,0:T(8,128)S(1)} collective-permute-done((f32[80,128]{1,0:T(8,128)S(1)}, f32[80,128]{1,0:T(8,128)S(1)}, u32[]{:S(2)}, u32[]{:S(2)}) %collective-permute-start.2) | collective-permute-done | bytes 40992 | tf_op jit(solution)/shard_map/ppermute | solution.py:291
  12.9 0.0 collective-permute-done.refs_1_
  12.9 4.0 %shard_map.69 = (f32[16,64,128]{2,1,0:T(8,128)S(1)}, f32[16,64,128]{2,1,0:T(8,128)S(1)}, f32[128,2,128]{2,1,0:T(2,128)S(1)}) custom-call(f32[5,64,256]{2,1,0:T(8,128)S(1)} %get-tuple-element.9.refs_0_.held_ref, f32[400,128]{1,0:T(8,128)S(1)} %collective-permute-done.refs_1_, f32[80,128]{1,0:T(8,128)S(1)} %collective-permute-done.1.refs_2_, ...), custom_call_target="tpu_custom_call" | custom-call | tf_op jit(solution)/shard_map/pallas_call | solution.py:263
  16.9 8.8 %collective-permute-start.3 = (f32[16,64,128]{2,1,0:T(8,128)S(1)}, f32[16,64,128]{2,1,0:T(8,128)S(1)}, u32[]{:S(2)}, u32[]{:S(2)}) collective-permute-start(f32[16,64,128]{2,1,0:T(8,128)S(1)} %get-tuple-element.15), channel_id=1, source_target_pairs={{0,64},{64,0},{1,65},{65,1},{2,66},{66,2},{3,67},{67,3},{4,68},{68... | collective-permute-start | bytes 1572872 | tf_op jit(solution)/shard_map/ppermute | solution.py:305
  25.7 12.9 %all_to_all.5.sums_ref = f32[128,2,128]{2,1,0:T(2,128)S(1)} all-to-all(f32[128,2,128]{2,1,0:T(2,128)S(1)} %get-tuple-element.13), channel_id=1, replica_groups=mesh['gx'=2,'gy_0'=4,'gy_1'=4,'gy_2'=4] {'gx','gy_0','gy_1','gy_2'}, dimensions={0} | all-to-all | bytes 262144 | tf_op jit(solution)/shard_map/all_to_all | solution.py:306
  38.6 0.0 collective-permute-done.3.got_ref
  38.6 1.4 %shard_map.70 = (f32[64,256]{1,0:T(8,128)}, f32[64,256]{1,0:T(8,128)}) custom-call(f32[128,2,128]{2,1,0:T(2,128)S(1)} %all_to_all.5.sums_ref, f32[16,64,128]{2,1,0:T(8,128)S(1)} %get-tuple-element.14.own_ref, f32[16,64,128]{2,1,0:T(8,128)S(1)} %collective-permute-done.3.got_ref, f32[5,64,256]{2,1,0:T(8,128)S(1)} %get-tuple-element.9.refs_0_.held_ref), custom_call_target="tpu_custom_call" | custom-call | tf_op jit(solution)/shard_map/pallas_call | solution.py:263
Async XLA Ops:
  1.8 11.1 %collective-permute-start = (f32[400,128]{1,0:T(8,128)S(1)}, f32[400,128]{1,0:T(8,128)S(1)}, u32[]{:S(2)}, u32[]{:S(2)}) collective-permute-start(f32[400,128]{1,0:T(8,128)S(1)} %get-tuple-element.10), channel_id=1, source_target_pairs={{0,64},{64,0},{1,65},{65,1},{2,66},{66,2},{3,67},{67,3},{4,68},{68... | collective-permute-start | bytes 614408 | tf_op jit(solution)/shard_map/ppermute | solution.py:293
  3.3 8.5 %collective-permute-start.1 = (f32[80,128]{1,0:T(8,128)S(1)}, f32[80,128]{1,0:T(8,128)S(1)}, u32[]{:S(2)}, u32[]{:S(2)}) collective-permute-start(f32[80,128]{1,0:T(8,128)S(1)} %get-tuple-element.11), channel_id=1, source_target_pairs={{0,127},{1,64},{2,65},{3,66},{4,67},{5,68},{6,69},{7,70},{8,71},{9... | collective-permute-start | bytes 122888 | tf_op jit(solution)/shard_map/ppermute | solution.py:292
  4.6 8.3 %collective-permute-start.2 = (f32[80,128]{1,0:T(8,128)S(1)}, f32[80,128]{1,0:T(8,128)S(1)}, u32[]{:S(2)}, u32[]{:S(2)}) collective-permute-start(f32[80,128]{1,0:T(8,128)S(1)} %get-tuple-element.12), channel_id=1, source_target_pairs={{0,1},{1,2},{2,3},{3,4},{4,5},{5,6},{6,7},{7,8},{8,9},{9,10},{10,1... | collective-permute-start | bytes 122888 | tf_op jit(solution)/shard_map/ppermute | solution.py:291
  16.9 21.7 %collective-permute-start.3 = (f32[16,64,128]{2,1,0:T(8,128)S(1)}, f32[16,64,128]{2,1,0:T(8,128)S(1)}, u32[]{:S(2)}, u32[]{:S(2)}) collective-permute-start(f32[16,64,128]{2,1,0:T(8,128)S(1)} %get-tuple-element.15), channel_id=1, source_target_pairs={{0,64},{64,0},{1,65},{65,1},{2,66},{66,2},{3,67},{67,3},{4,68},{68... | collective-permute-start | bytes 1572872 | tf_op jit(solution)/shard_map/ppermute | solution.py:305

commit v7 on v6

--- a/solution.py
+++ b/solution.py
@@ -177,24 +177,20 @@
 
     for low in range(0, 16, 4):
         for high in range(low, 16, 4):
+            wanted = [(i, k) for i in range(4) for k in range(4) if low != high or i <= k]
 
             def accumulate(t, sums):
                 rows = pl.ds(pl.multiple_of(8 * t, 8), 8)
                 first = [image[low + i, rows, :] for i in range(4)]
                 second = first if low == high else [image[high + i, rows, :] for i in range(4)]
-                return tuple(sums[4 * i + k] + first[i] * second[k] for i in range(4) for k in range(4))
-
-            sums = lax.fori_loop(
-                0, FULL // 8, accumulate, tuple(jnp.zeros((8, LANES), jnp.float32) for _ in range(16)), unroll=8
-            )
-            for i in range(4):
-                for k in range(4):
-                    row = jnp.sum(sums[4 * i + k], axis=0, keepdims=True)
-                    at = 16 * (low + i) + high + k
+                return tuple(total + first[i] * second[k] for total, (i, k) in zip(sums, wanted))
+
+            zeros = tuple(jnp.zeros((8, LANES), jnp.float32) for _ in wanted)
+            sums = lax.fori_loop(0, FULL // 8, accumulate, zeros, unroll=16)
+            for total, (i, k) in zip(sums, wanted):
+                row = jnp.sum(total, axis=0, keepdims=True)
+                for at in sorted({16 * (low + i) + high + k, 16 * (high + k) + low + i}):
                     pairs[at : at + 1, :] = row
-                    if low != high:
-                        at = 16 * (high + k) + low + i
-                        pairs[at : at + 1, :] = row
     total = lax.dot_general(
         jnp.ones((8, LANES), jnp.float32),
         pairs[...],
@@ -207,7 +203,7 @@
 
 
 def finish_body(sums_ref, own_ref, got_ref, held_ref, solution_ref, residual_ref):
-    total = jnp.sum(sums_ref[...], axis=0)
+    total = jnp.sum(jnp.sum(sums_ref[...].reshape(-1, 8, 2, LANES), axis=0), axis=0)
     total = jnp.concatenate([total[0:1], total[1:2]], axis=1)
     lane = lax.broadcasted_iota(jnp.int32, (16, COLS), 1)
     sub = lax.broadcasted_iota(jnp.int32, (16, COLS), 0)

time: 40.2 us -> 40 us (level)
  no operation moved by 1% of the time
where the time goes in v7:
time: 40 us; the launch traced here: 39.8 us
  starting transfers between devices  18.8 us (47%)
  blocking collectives  12.9 us (32%)
  Pallas kernels  6.35 us (16%)
  waiting for transfers between devices  1.11 us (3%)
  between operations  0.65 us (2%)
    all_to_all x1, blocking collectives, per_device(): sums = lax.all_to_all(gram, ALL, 0, 0, tiled=True)  12.9 us
    ppermute x1, starting transfers between devices, per_device(): got = lax.ppermute(give, 'gx', swap)  8.8 us
    ppermute x1, starting transfers between devices, per_device(): from_same = lax.ppermute(to_same, ALL, same)  7.22 us
    pallas_call x3, Pallas kernels, run(): pl.pallas_call(body, out_shape=out_shape, in_specs=[vmem] * len(args), ou...  6.35 us
    ppermute x1, starting transfers between devices, per_device(): from_partner = lax.ppermute(to_partner, 'gx', swap)  1.47 us
    ppermute x1, starting transfers between devices, per_device(): from_cross = lax.ppermute(to_cross, ALL, cross)  1.3 us
    ppermute x1, waiting for transfers between devices, per_device(): from_same = lax.ppermute(to_same, ALL, same)  1.1 us
  transfers between devices with their start and end apart: 4, of which 1 were waited for; matrix products, arithmetic and copies ran while one was open for 0% of the time, Pallas kernels for 0%

profile of v7, /device:TPU:1, one launch (start us, length us, event | category | flops | bytes accessed | tf_op | source)
XLA Modules:
  0.0 39.8 jit_solution(4025206273269261110)
XLA Ops:
  0.6 1.1 %shard_map.68 = (f32[80,128]{1,0:T(8,128)S(1)}, f32[80,128]{1,0:T(8,128)S(1)}, f32[400,128]{1,0:T(8,128)S(1)}, f32[5,64,256]{2,1,0:T(8,128)S(1)}) custom-call(f32[64,256]{1,0:T(8,128)} %refs_0_.1, f32[64,256]{1,0:T(8,128)} %refs_1_.1, f32[64,256]{1,0:T(8,128)} %refs_2_.1, f32[64,256]{1,0:T(8,128)} %refs_3_.1, f32[64,256]{1,0:T(8,128)} %refs_4_.1), custom_call_target="tpu_custom_call" | custom-call | tf_op jit(solution)/shard_map/pallas_call | solution.py:259
  1.8 1.5 %collective-permute-start = (f32[400,128]{1,0:T(8,128)S(1)}, f32[400,128]{1,0:T(8,128)S(1)}, u32[]{:S(2)}, u32[]{:S(2)}) collective-permute-start(f32[400,128]{1,0:T(8,128)S(1)} %get-tuple-element.10), channel_id=1, source_target_pairs={{0,64},{64,0},{1,65},{65,1},{2,66},{66,2},{3,67},{67,3},{4,68},{68... | collective-permute-start | bytes 614408 | tf_op jit(solution)/shard_map/ppermute | solution.py:289
  3.3 1.3 %collective-permute-start.1 = (f32[80,128]{1,0:T(8,128)S(1)}, f32[80,128]{1,0:T(8,128)S(1)}, u32[]{:S(2)}, u32[]{:S(2)}) collective-permute-start(f32[80,128]{1,0:T(8,128)S(1)} %get-tuple-element.11), channel_id=1, source_target_pairs={{0,127},{1,64},{2,65},{3,66},{4,67},{5,68},{6,69},{7,70},{8,71},{9... | collective-permute-start | bytes 122888 | tf_op jit(solution)/shard_map/ppermute | solution.py:288
  4.6 7.2 %collective-permute-start.2 = (f32[80,128]{1,0:T(8,128)S(1)}, f32[80,128]{1,0:T(8,128)S(1)}, u32[]{:S(2)}, u32[]{:S(2)}) collective-permute-start(f32[80,128]{1,0:T(8,128)S(1)} %get-tuple-element.12), channel_id=1, source_target_pairs={{0,1},{1,2},{2,3},{3,4},{4,5},{5,6},{6,7},{7,8},{8,9},{9,10},{10,1... | collective-permute-start | bytes 122888 | tf_op jit(solution)/shard_map/ppermute | solution.py:287
  11.8 0.0 collective-permute-done.1.refs_2_
  11.8 1.1 %collective-permute-done.2.refs_3_ = f32[80,128]{1,0:T(8,128)S(1)} collective-permute-done((f32[80,128]{1,0:T(8,128)S(1)}, f32[80,128]{1,0:T(8,128)S(1)}, u32[]{:S(2)}, u32[]{:S(2)}) %collective-permute-start.2) | collective-permute-done | bytes 40992 | tf_op jit(solution)/shard_map/ppermute | solution.py:287
  12.9 0.0 collective-permute-done.refs_1_
  12.9 3.9 %shard_map.69 = (f32[16,64,128]{2,1,0:T(8,128)S(1)}, f32[16,64,128]{2,1,0:T(8,128)S(1)}, f32[128,2,128]{2,1,0:T(2,128)S(1)}) custom-call(f32[5,64,256]{2,1,0:T(8,128)S(1)} %get-tuple-element.9.refs_0_.held_ref, f32[400,128]{1,0:T(8,128)S(1)} %collective-permute-done.refs_1_, f32[80,128]{1,0:T(8,128)S(1)} %collective-permute-done.1.refs_2_, ...), custom_call_target="tpu_custom_call" | custom-call | tf_op jit(solution)/shard_map/pallas_call | solution.py:259
  16.8 8.8 %collective-permute-start.3 = (f32[16,64,128]{2,1,0:T(8,128)S(1)}, f32[16,64,128]{2,1,0:T(8,128)S(1)}, u32[]{:S(2)}, u32[]{:S(2)}) collective-permute-start(f32[16,64,128]{2,1,0:T(8,128)S(1)} %get-tuple-element.15), channel_id=1, source_target_pairs={{0,64},{64,0},{1,65},{65,1},{2,66},{66,2},{3,67},{67,3},{4,68},{68... | collective-permute-start | bytes 1572872 | tf_op jit(solution)/shard_map/ppermute | solution.py:301
  25.6 12.9 %all_to_all.5.sums_ref = f32[128,2,128]{2,1,0:T(2,128)S(1)} all-to-all(f32[128,2,128]{2,1,0:T(2,128)S(1)} %get-tuple-element.13), channel_id=1, replica_groups=mesh['gx'=2,'gy_0'=4,'gy_1'=4,'gy_2'=4] {'gx','gy_0','gy_1','gy_2'}, dimensions={0} | all-to-all | bytes 262144 | tf_op jit(solution)/shard_map/all_to_all | solution.py:302
  38.5 0.0 collective-permute-done.3.got_ref
  38.5 1.3 %shard_map.70 = (f32[64,256]{1,0:T(8,128)}, f32[64,256]{1,0:T(8,128)}) custom-call(f32[128,2,128]{2,1,0:T(2,128)S(1)} %all_to_all.5.sums_ref, f32[16,64,128]{2,1,0:T(8,128)S(1)} %get-tuple-element.14.own_ref, f32[16,64,128]{2,1,0:T(8,128)S(1)} %collective-permute-done.3.got_ref, f32[5,64,256]{2,1,0:T(8,128)S(1)} %get-tuple-element.9.refs_0_.held_ref), custom_call_target="tpu_custom_call" | custom-call | tf_op jit(solution)/shard_map/pallas_call | solution.py:259
Async XLA Ops:
  1.8 11.1 %collective-permute-start = (f32[400,128]{1,0:T(8,128)S(1)}, f32[400,128]{1,0:T(8,128)S(1)}, u32[]{:S(2)}, u32[]{:S(2)}) collective-permute-start(f32[400,128]{1,0:T(8,128)S(1)} %get-tuple-element.10), channel_id=1, source_target_pairs={{0,64},{64,0},{1,65},{65,1},{2,66},{66,2},{3,67},{67,3},{4,68},{68... | collective-permute-start | bytes 614408 | tf_op jit(solution)/shard_map/ppermute | solution.py:289
  3.3 8.5 %collective-permute-start.1 = (f32[80,128]{1,0:T(8,128)S(1)}, f32[80,128]{1,0:T(8,128)S(1)}, u32[]{:S(2)}, u32[]{:S(2)}) collective-permute-start(f32[80,128]{1,0:T(8,128)S(1)} %get-tuple-element.11), channel_id=1, source_target_pairs={{0,127},{1,64},{2,65},{3,66},{4,67},{5,68},{6,69},{7,70},{8,71},{9... | collective-permute-start | bytes 122888 | tf_op jit(solution)/shard_map/ppermute | solution.py:288
  4.6 8.3 %collective-permute-start.2 = (f32[80,128]{1,0:T(8,128)S(1)}, f32[80,128]{1,0:T(8,128)S(1)}, u32[]{:S(2)}, u32[]{:S(2)}) collective-permute-start(f32[80,128]{1,0:T(8,128)S(1)} %get-tuple-element.12), channel_id=1, source_target_pairs={{0,1},{1,2},{2,3},{3,4},{4,5},{5,6},{6,7},{7,8},{8,9},{9,10},{10,1... | collective-permute-start | bytes 122888 | tf_op jit(solution)/shard_map/ppermute | solution.py:287
  16.8 21.7 %collective-permute-start.3 = (f32[16,64,128]{2,1,0:T(8,128)S(1)}, f32[16,64,128]{2,1,0:T(8,128)S(1)}, u32[]{:S(2)}, u32[]{:S(2)}) collective-permute-start(f32[16,64,128]{2,1,0:T(8,128)S(1)} %get-tuple-element.15), channel_id=1, source_target_pairs={{0,64},{64,0},{1,65},{65,1},{2,66},{66,2},{3,67},{67,3},{4,68},{68... | collective-permute-start | bytes 1572872 | tf_op jit(solution)/shard_map/ppermute | solution.py:301

commit v8 on v6

--- a/solution.py
+++ b/solution.py
@@ -173,7 +173,7 @@
             wrap(later, 0)
         return carried
 
-    lax.fori_loop(0, RESTART // 3, steps, 0)
+    lax.fori_loop(0, RESTART // 3, steps, 0, unroll=RESTART // 3)
 
     for low in range(0, 16, 4):
         for high in range(low, 16, 4):
@@ -185,7 +185,7 @@
                 return tuple(sums[4 * i + k] + first[i] * second[k] for i in range(4) for k in range(4))
 
             sums = lax.fori_loop(
-                0, FULL // 8, accumulate, tuple(jnp.zeros((8, LANES), jnp.float32) for _ in range(16)), unroll=8
+                0, FULL // 8, accumulate, tuple(jnp.zeros((8, LANES), jnp.float32) for _ in range(16)), unroll=16
             )
             for i in range(4):
                 for k in range(4):
@@ -207,7 +207,7 @@
 
 
 def finish_body(sums_ref, own_ref, got_ref, held_ref, solution_ref, residual_ref):
-    total = jnp.sum(sums_ref[...], axis=0)
+    total = jnp.sum(jnp.sum(sums_ref[...].reshape(-1, 8, 2, LANES), axis=0), axis=0)
     total = jnp.concatenate([total[0:1], total[1:2]], axis=1)
     lane = lax.broadcasted_iota(jnp.int32, (16, COLS), 1)
     sub = lax.broadcasted_iota(jnp.int32, (16, COLS), 0)

time: 40.2 us -> 39.7 us (0.988)
  Pallas kernels: 6.5 us -> 6.04 us
    pallas_call x3, Pallas kernels: 6.5 us -> 6.04 us  [run(): pl.pallas_call(body, out_shape=out_shape, in_specs=[vmem] * len(args), ou...]
where the time goes in v8:
time: 39.7 us; the launch traced here: 39.5 us
  starting transfers between devices  18.8 us (47%)
  blocking collectives  12.9 us (32%)
  Pallas kernels  6.04 us (15%)
  waiting for transfers between devices  1.11 us (3%)
  between operations  0.65 us (2%)
    all_to_all x1, blocking collectives, per_device(): sums = lax.all_to_all(gram, ALL, 0, 0, tiled=True)  12.9 us
    ppermute x1, starting transfers between devices, per_device(): got = lax.ppermute(give, 'gx', swap)  8.8 us
    ppermute x1, starting transfers between devices, per_device(): from_same = lax.ppermute(to_same, ALL, same)  7.22 us
    pallas_call x3, Pallas kernels, run(): pl.pallas_call(body, out_shape=out_shape, in_specs=[vmem] * len(args), ou...  6.04 us
    ppermute x1, starting transfers between devices, per_device(): from_partner = lax.ppermute(to_partner, 'gx', swap)  1.47 us
    ppermute x1, starting transfers between devices, per_device(): from_cross = lax.ppermute(to_cross, ALL, cross)  1.3 us
    ppermute x1, waiting for transfers between devices, per_device(): from_same = lax.ppermute(to_same, ALL, same)  1.1 us
  transfers between devices with their start and end apart: 4, of which 1 were waited for; matrix products, arithmetic and copies ran while one was open for 0% of the time, Pallas kernels for 0%

profile of v8, /device:TPU:1, one launch (start us, length us, event | category | flops | bytes accessed | tf_op | source)
XLA Modules:
  0.0 39.5 jit_solution(2970088594585644744)
XLA Ops:
  0.6 1.1 %shard_map.68 = (f32[80,128]{1,0:T(8,128)S(1)}, f32[80,128]{1,0:T(8,128)S(1)}, f32[400,128]{1,0:T(8,128)S(1)}, f32[5,64,256]{2,1,0:T(8,128)S(1)}) custom-call(f32[64,256]{1,0:T(8,128)} %refs_0_.1, f32[64,256]{1,0:T(8,128)} %refs_1_.1, f32[64,256]{1,0:T(8,128)} %refs_2_.1, f32[64,256]{1,0:T(8,128)} %refs_3_.1, f32[64,256]{1,0:T(8,128)} %refs_4_.1), custom_call_target="tpu_custom_call" | custom-call | tf_op jit(solution)/shard_map/pallas_call | solution.py:263
  1.8 1.5 %collective-permute-start = (f32[400,128]{1,0:T(8,128)S(1)}, f32[400,128]{1,0:T(8,128)S(1)}, u32[]{:S(2)}, u32[]{:S(2)}) collective-permute-start(f32[400,128]{1,0:T(8,128)S(1)} %get-tuple-element.10), channel_id=1, source_target_pairs={{0,64},{64,0},{1,65},{65,1},{2,66},{66,2},{3,67},{67,3},{4,68},{68... | collective-permute-start | bytes 614408 | tf_op jit(solution)/shard_map/ppermute | solution.py:293
  3.3 1.3 %collective-permute-start.1 = (f32[80,128]{1,0:T(8,128)S(1)}, f32[80,128]{1,0:T(8,128)S(1)}, u32[]{:S(2)}, u32[]{:S(2)}) collective-permute-start(f32[80,128]{1,0:T(8,128)S(1)} %get-tuple-element.11), channel_id=1, source_target_pairs={{0,127},{1,64},{2,65},{3,66},{4,67},{5,68},{6,69},{7,70},{8,71},{9... | collective-permute-start | bytes 122888 | tf_op jit(solution)/shard_map/ppermute | solution.py:292
  4.6 7.2 %collective-permute-start.2 = (f32[80,128]{1,0:T(8,128)S(1)}, f32[80,128]{1,0:T(8,128)S(1)}, u32[]{:S(2)}, u32[]{:S(2)}) collective-permute-start(f32[80,128]{1,0:T(8,128)S(1)} %get-tuple-element.12), channel_id=1, source_target_pairs={{0,1},{1,2},{2,3},{3,4},{4,5},{5,6},{6,7},{7,8},{8,9},{9,10},{10,1... | collective-permute-start | bytes 122888 | tf_op jit(solution)/shard_map/ppermute | solution.py:291
  11.8 0.0 collective-permute-done.1.refs_2_
  11.8 1.1 %collective-permute-done.2.refs_3_ = f32[80,128]{1,0:T(8,128)S(1)} collective-permute-done((f32[80,128]{1,0:T(8,128)S(1)}, f32[80,128]{1,0:T(8,128)S(1)}, u32[]{:S(2)}, u32[]{:S(2)}) %collective-permute-start.2) | collective-permute-done | bytes 40992 | tf_op jit(solution)/shard_map/ppermute | solution.py:291
  12.9 0.0 collective-permute-done.refs_1_
  12.9 3.6 %shard_map.69 = (f32[16,64,128]{2,1,0:T(8,128)S(1)}, f32[16,64,128]{2,1,0:T(8,128)S(1)}, f32[128,2,128]{2,1,0:T(2,128)S(1)}) custom-call(f32[5,64,256]{2,1,0:T(8,128)S(1)} %get-tuple-element.9.refs_0_.held_ref, f32[400,128]{1,0:T(8,128)S(1)} %collective-permute-done.refs_1_, f32[80,128]{1,0:T(8,128)S(1)} %collective-permute-done.1.refs_2_, ...), custom_call_target="tpu_custom_call" | custom-call | tf_op jit(solution)/shard_map/pallas_call | solution.py:263
  16.5 8.8 %collective-permute-start.3 = (f32[16,64,128]{2,1,0:T(8,128)S(1)}, f32[16,64,128]{2,1,0:T(8,128)S(1)}, u32[]{:S(2)}, u32[]{:S(2)}) collective-permute-start(f32[16,64,128]{2,1,0:T(8,128)S(1)} %get-tuple-element.15), channel_id=1, source_target_pairs={{0,64},{64,0},{1,65},{65,1},{2,66},{66,2},{3,67},{67,3},{4,68},{68... | collective-permute-start | bytes 1572872 | tf_op jit(solution)/shard_map/ppermute | solution.py:305
  25.3 12.9 %all_to_all.5.sums_ref = f32[128,2,128]{2,1,0:T(2,128)S(1)} all-to-all(f32[128,2,128]{2,1,0:T(2,128)S(1)} %get-tuple-element.13), channel_id=1, replica_groups=mesh['gx'=2,'gy_0'=4,'gy_1'=4,'gy_2'=4] {'gx','gy_0','gy_1','gy_2'}, dimensions={0} | all-to-all | bytes 262144 | tf_op jit(solution)/shard_map/all_to_all | solution.py:306
  38.2 0.0 collective-permute-done.3.got_ref
  38.2 1.3 %shard_map.70 = (f32[64,256]{1,0:T(8,128)}, f32[64,256]{1,0:T(8,128)}) custom-call(f32[128,2,128]{2,1,0:T(2,128)S(1)} %all_to_all.5.sums_ref, f32[16,64,128]{2,1,0:T(8,128)S(1)} %get-tuple-element.14.own_ref, f32[16,64,128]{2,1,0:T(8,128)S(1)} %collective-permute-done.3.got_ref, f32[5,64,256]{2,1,0:T(8,128)S(1)} %get-tuple-element.9.refs_0_.held_ref), custom_call_target="tpu_custom_call" | custom-call | tf_op jit(solution)/shard_map/pallas_call | solution.py:263
Async XLA Ops:
  1.8 11.1 %collective-permute-start = (f32[400,128]{1,0:T(8,128)S(1)}, f32[400,128]{1,0:T(8,128)S(1)}, u32[]{:S(2)}, u32[]{:S(2)}) collective-permute-start(f32[400,128]{1,0:T(8,128)S(1)} %get-tuple-element.10), channel_id=1, source_target_pairs={{0,64},{64,0},{1,65},{65,1},{2,66},{66,2},{3,67},{67,3},{4,68},{68... | collective-permute-start | bytes 614408 | tf_op jit(solution)/shard_map/ppermute | solution.py:293
  3.3 8.5 %collective-permute-start.1 = (f32[80,128]{1,0:T(8,128)S(1)}, f32[80,128]{1,0:T(8,128)S(1)}, u32[]{:S(2)}, u32[]{:S(2)}) collective-permute-start(f32[80,128]{1,0:T(8,128)S(1)} %get-tuple-element.11), channel_id=1, source_target_pairs={{0,127},{1,64},{2,65},{3,66},{4,67},{5,68},{6,69},{7,70},{8,71},{9... | collective-permute-start | bytes 122888 | tf_op jit(solution)/shard_map/ppermute | solution.py:292
  4.6 8.3 %collective-permute-start.2 = (f32[80,128]{1,0:T(8,128)S(1)}, f32[80,128]{1,0:T(8,128)S(1)}, u32[]{:S(2)}, u32[]{:S(2)}) collective-permute-start(f32[80,128]{1,0:T(8,128)S(1)} %get-tuple-element.12), channel_id=1, source_target_pairs={{0,1},{1,2},{2,3},{3,4},{4,5},{5,6},{6,7},{7,8},{8,9},{9,10},{10,1... | collective-permute-start | bytes 122888 | tf_op jit(solution)/shard_map/ppermute | solution.py:291
  16.5 21.7 %collective-permute-start.3 = (f32[16,64,128]{2,1,0:T(8,128)S(1)}, f32[16,64,128]{2,1,0:T(8,128)S(1)}, u32[]{:S(2)}, u32[]{:S(2)}) collective-permute-start(f32[16,64,128]{2,1,0:T(8,128)S(1)} %get-tuple-element.15), channel_id=1, source_target_pairs={{0,64},{64,0},{1,65},{65,1},{2,66},{66,2},{3,67},{67,3},{4,68},{68... | collective-permute-start | bytes 1572872 | tf_op jit(solution)/shard_map/ppermute | solution.py:305
